TPU v7x, 256 devices: a whole 4x4x8 slice. The times are simulated.
256 devices in a mesh: mp: 64 (over y, z, core), dp: 4 (over x).
Axes of the slice: x: 4, y: 4, z: 8, core: 2. Of those that a mesh axis runs over, the one named last changes fastest.
Arguments:
- features: bfloat16 [256, 4, 4, 512], P(('dp', 'mp')), may hold values from 0 to 2
- labels: int32 [256], P('dp'), may hold values from 0 to 9
- subset_ids: int32 [64], P('mp'), may hold values from 0 to 255
- conv1_weight: bfloat16 [64, 9, 512, 512], P('mp'), may hold values from -0.09375 to 0.09375
- conv2_weight: bfloat16 [64, 9, 512, 512], P('mp'), may hold values from -0.09375 to 0.09375
- head_weight: float32 [64, 512, 10], P('mp'), may hold values from -0.25 to 0.25
Outputs:
- datamodel: float32 [256, 256], P(('dp', 'mp'))
- margin_mean: float32 [256], P(('dp', 'mp'))
- margin_norm: float32 [256], P(('dp', 'mp'))
All inputs are finite; a program needn't handle non-finite values.
Results may differ from a plain program's by a relative error of at most 0.00077.
Values may be sent and summed in bfloat16 or wider, within the bound.
No kernel may reach another device: no remote copies, remote signals or barrier semaphores. Data moves between devices by JAX's collectives and lax.ppermute only.
A program may use at most 128 MiB of HBM per device.

v0:
```python
import functools

import jax
import jax.numpy as jnp
from jax import lax
from jax.experimental import pallas as pl
from jax.experimental.pallas import tpu as pltpu
from jax.sharding import Mesh, PartitionSpec as P


SIDE = 4
SPOTS = SIDE * SIDE
HALF = 256
CLASSES = 10
SUBSETS = 256
GROUP = 16

OFFSETS = (0, 1, 2, 3, 5, 6, 7, 8, 4)


def pairs_of(offset):
    row_off, col_off = offset // 3 - 1, offset % 3 - 1
    return [
        (r * SIDE + c, (r + row_off) * SIDE + c + col_off)
        for r in range(SIDE)
        for c in range(SIDE)
        if 0 <= r + row_off < SIDE and 0 <= c + col_off < SIDE
    ]


def convolve(source, weight, accs):
    stage = 0
    for offset in OFFSETS:
        pairs = pairs_of(offset)
        for k in range(2):
            deep = pl.ds(k * HALF, HALF)
            for n in range(2):
                pltpu.matmul_push_rhs(
                    weight[offset, deep, pl.ds(n * HALF, HALF)], staging_register=stage, mxu_index=n
                )
            for i, (spot, origin) in enumerate(pairs):
                rows = source[origin, :, deep]
                for n in range(2):
                    pltpu.matmul_acc_lhs(
                        accs[n][spot], rows, load_staged_rhs=stage if i == 0 else None
                    )
            stage = 1 - stage


def by_position(sources, moved, accs):
    lane = lax.broadcasted_iota(jnp.int32, (GROUP, HALF), 1)
    target = lax.broadcasted_iota(jnp.int32, (GROUP, HALF), 0)
    picks = [
        jnp.where(lane == target * SPOTS + spot, 1.0, 0.0).astype(jnp.bfloat16)
        for spot in range(SPOTS)
    ]
    pick = jnp.concatenate(picks, axis=0)
    for g, refs in enumerate(sources):
        for n in range(2):
            block = [ref[:, :, pl.ds(n * HALF, HALF)].reshape(-1, HALF) for ref in refs]
            pltpu.matmul_push_rhs(
                jnp.concatenate(block, axis=0), staging_register=g % 2, mxu_index=n
            )
            pltpu.matmul_acc_lhs(accs[n][g], pick, load_staged_rhs=g % 2)
    for g in range(len(sources)):
        for n in range(2):
            got = pltpu.matmul_pop(accs[n][g]).astype(jnp.bfloat16)
            moved[:, pl.ds(g * GROUP, GROUP), pl.ds(n * HALF, HALF)] = got.reshape(SPOTS, GROUP, HALF)


def conv_kernel(columns, *refs):
    labels, head, w1, w2 = refs[:4]
    grids = refs[4 : 4 + len(columns)]
    ident = refs[5 + len(columns)] if len(refs) == 10 + len(columns) else None
    out, moved, hidden, pooled = refs[-4:]
    targets = moved.shape[1]
    deep = grids[0].shape[0]
    groups = targets // GROUP
    sources = [grids[2 * g : 2 * g + 2] for g in range(groups)]

    def shuffle(*flat):
        by_position(sources, moved, (flat[:groups], flat[groups:]))

    pl.run_scoped(
        shuffle,
        *[pltpu.ACC(n)((HALF, HALF), jnp.float32) for n in range(2) for _ in range(groups)],
    )

    def both(*flat):
        accs = (flat[:SPOTS], flat[SPOTS:])
        convolve(moved, w1, accs)
        for spot in range(SPOTS):
            for n in range(2):
                got = jnp.maximum(pltpu.matmul_pop(accs[n][spot]), 0.0)
                hidden[spot, :, pl.ds(n * HALF, HALF)] = got.astype(jnp.bfloat16)
        convolve(hidden, w2, accs)
        for spot in range(SPOTS):
            for n in range(2):
                cols = pl.ds(n * HALF, HALF)
                got = jnp.maximum(pltpu.matmul_pop(accs[n][spot]), 0.0)
                got = got + moved[spot, :, cols].astype(jnp.float32)
                if spot:
                    got = jnp.maximum(got, pooled[:, cols])
                pooled[:, cols] = got

    pl.run_scoped(
        both,
        *[pltpu.ACC(n)((targets, HALF), jnp.float32) for n in range(2) for _ in range(SPOTS)],
    )

    core, y = lax.axis_index("core"), lax.axis_index("y")
    firsts = []
    for mask, swap in columns:
        first = lax.bitwise_xor(y, jnp.int32(mask)) * (2 * deep)
        firsts.append(first + (1 - core if swap else core))
    wide = (targets, 128)
    lane = lax.broadcasted_iota(jnp.int32, wide, 1)
    line = lax.broadcasted_iota(jnp.int32, wide, 0)
    place = 2 * (line & (deep - 1))
    for i, first in enumerate(firsts):
        place = place + jnp.where(line // deep == i, first, 0)
    few = labels.shape[1]
    spread_labels = jnp.broadcast_to(labels[...].astype(jnp.float32), (targets, few))
    mine = jnp.where(place[:, :few] == lane[:, :few], spread_labels, 0.0)
    label = jnp.sum(mine, axis=1, keepdims=True).astype(jnp.int32)
    logits = jnp.full(wide, -1e30, jnp.float32)
    for k in range(CLASSES):
        total = pooled[:, pl.ds(0, 128)] * head[k, :, pl.ds(0, 128)]
        for j in range(1, 4):
            cols = pl.ds(j * 128, 128)
            total = total + pooled[:, cols] * head[k, :, cols]
        logits = jnp.where(lane == k, jnp.sum(total, axis=1, keepdims=True), logits)
    chosen = lane == label
    correct = jnp.sum(jnp.where(chosen, logits, 0.0), axis=1, keepdims=True)
    rival = jnp.max(jnp.where(chosen, -1e30, logits), axis=1, keepdims=True)
    packed = jnp.broadcast_to(correct - rival, wide)
    for i in range(targets):
        out[pl.ds(firsts[i // deep] + 2 * (i % deep), 1), 0, :] = packed[i : i + 1, :]
    if ident is not None:
        whole = out[...]
        low = lax.broadcasted_iota(jnp.int32, whole.shape, 2) < 64
        out[...] = jnp.where(low, whole, ident[0].astype(jnp.float32))


def in_vmem(x):
    return pltpu.with_memory_space_constraint(x, pltpu.VMEM)


def conv_call(columns, grids, labels, head, w1, w2, before=None, ident=None):
    targets = sum(grid.shape[0] for grid in grids)
    vmem = pl.BlockSpec(memory_space=pltpu.VMEM)
    operands = [labels, head, *map(in_vmem, (w1, w2, *grids))]
    specs = [vmem] * len(operands)
    aliases = {}
    if before is not None:
        aliases = {len(operands): 0}
        operands.append(in_vmem(before))
        specs.append(vmem)
    if ident is not None:
        operands.append(ident)
        specs.append(pl.BlockSpec(memory_space=pltpu.SMEM))
    work = 2 * 100 * targets * 512 * 512 * 2
    return pl.pallas_call(
        functools.partial(conv_kernel, columns),
        out_shape=pltpu.VMEM((64, 1, 128), jnp.float32),
        in_specs=specs,
        out_specs=vmem,
        scratch_shapes=[
            pltpu.VMEM((SPOTS, targets, 512), jnp.bfloat16),
            pltpu.VMEM((SPOTS, targets, 512), jnp.bfloat16),
            pltpu.VMEM((targets, 512), jnp.float32),
        ],
        input_output_aliases=aliases,
        cost_estimate=pl.CostEstimate(flops=work, bytes_accessed=1 << 20, transcendentals=0),
        compiler_params=pltpu.CompilerParams(vmem_limit_bytes=16 * 1024 * 1024),
    )(*operands)


def spread_kernel(grid, out):
    flat = grid[...].reshape(SPOTS, grid.shape[-1])
    for i in range(out.shape[0]):
        out[i] = flat


def spread_call(grid, copies):
    return pl.pallas_call(
        spread_kernel,
        out_shape=pltpu.VMEM((copies, SPOTS, grid.shape[-1]), grid.dtype),
        in_specs=[pl.BlockSpec(memory_space=pltpu.VMEM)],
        out_specs=pl.BlockSpec(memory_space=pltpu.VMEM),
        cost_estimate=pl.CostEstimate(flops=10**10, bytes_accessed=1 << 25, transcendentals=0),
        compiler_params=pltpu.CompilerParams(vmem_limit_bytes=1024 * 1024),
        name="spread",
    )(grid)


def tail_kernel(columns, datamodel, mean_out, norm_out):
    models = columns.shape[0]
    rows = columns[:, 0, :]
    lane = lax.broadcasted_iota(jnp.int32, rows.shape, 1)
    margin = jnp.max(jnp.where(lane < 64, rows, -3e38), axis=1, keepdims=True)
    ident = jnp.max(jnp.where(lane < 64, -1.0, rows), axis=1, keepdims=True)
    mean = jnp.sum(margin, axis=0, keepdims=True) / models
    centred = margin - mean
    norm = jnp.sqrt(1.0 + jnp.sum(centred * centred, axis=0, keepdims=True) / models)
    scaled = centred / norm
    subset = lax.broadcasted_iota(jnp.int32, (models, SUBSETS), 1).astype(jnp.float32)
    datamodel[...] = jnp.sum(jnp.where(subset == ident, scaled, 0.0), axis=0, keepdims=True)
    mean_out[...] = jnp.broadcast_to(mean, mean_out.shape)
    norm_out[...] = jnp.broadcast_to(norm, norm_out.shape)


def tail_call(columns):
    vmem = pl.BlockSpec(memory_space=pltpu.VMEM)
    return pl.pallas_call(
        tail_kernel,
        out_shape=(
            jax.ShapeDtypeStruct((1, SUBSETS), jnp.float32),
            jax.ShapeDtypeStruct((1, 128), jnp.float32),
            jax.ShapeDtypeStruct((1, 128), jnp.float32),
        ),
        in_specs=[vmem],
        out_specs=(vmem, vmem, vmem),
        compiler_params=pltpu.CompilerParams(vmem_limit_bytes=1024 * 1024),
        name="statistics",
    )(columns)


def exchanged(x, axis):
    return lax.all_to_all(x, axis, 0, 0, tiled=True)


def swapped(x, axis, mask):
    return lax.ppermute(x, axis, [(i, i ^ mask) for i in range(lax.axis_size(axis))])


def staged(features, labels, subset_ids, conv1_weight, conv2_weight, head_weight):
    column = exchanged(spread_call(features[0], lax.axis_size("z")), "z")
    head = jnp.transpose(head_weight, (2, 0, 1))
    fixed = (labels.reshape(1, -1), head, conv1_weight[0], conv2_weight[0])
    column_o = swapped(column, "core", 1)
    near = swapped(column, "y", 3)
    next_ = swapped(column, "y", 1)
    far = swapped(column, "y", 2)
    packed = conv_call(((0, False), (0, True)), (column, column_o), *fixed)
    near, next_, packed = lax.optimization_barrier((near, next_, packed))
    near_o, next_o = swapped(near, "core", 1), swapped(next_, "core", 1)
    packed = conv_call(((3, False), (1, False)), (near, next_), *fixed, packed)
    far, packed = lax.optimization_barrier((far, packed))
    far_o = swapped(far, "core", 1)
    packed = conv_call(((3, True), (1, True)), (near_o, next_o), *fixed, packed)
    ident, packed = lax.optimization_barrier((subset_ids, packed))
    packed = conv_call(((2, False), (2, True)), (far, far_o), *fixed, packed, ident)
    columns = exchanged(packed, ("y", "z", "core"))
    datamodel, mean, norm = tail_call(columns)
    return (datamodel, mean[0, :1], norm[0, :1])


def solution(mesh):
    fine = Mesh(mesh.devices.reshape(4, 8, 2, 4), ("y", "z", "core", "dp"))
    mp = ("y", "z", "core")
    every = ("dp", *mp)
    in_specs = (
        P(every, None, None, None),
        P("dp"),
        P(mp),
        P(mp, None, None, None),
        P(mp, None, None, None),
        P(mp, None, None),
    )
    out_specs = (P(every, None), P(every), P(every))
    return jax.shard_map(staged, mesh=fine, in_specs=in_specs, out_specs=out_specs, check_vma=False)
```

profile of v0, /device:TPU:1, one launch (start us, length us, event | category | flops | bytes accessed | tf_op | source)
XLA Modules:
  0.0 51.8 jit_solution(5638667884929186858)
XLA Ops:
  0.6 0.0 copy-start.4
  0.6 0.7 %copy-done.4 = bf16[1,4,4,512]{3,2,1,0:T(4,128)(2,1)S(1)} copy-done((bf16[1,4,4,512]{3,2,1,0:T(4,128)(2,1)S(1)}, bf16[1,4,4,512]{3,2,1,0:T(4,128)(2,1)}, u32[]{:S(2)}) %copy-start.4) | copy-done | bytes 16408
  1.4 0.0 copy-start
  1.4 0.0 copy-start.1
  1.4 0.0 copy-start.2
  1.4 0.0 copy-start.3
  1.4 16.8 %all_to_all.10.refs_4_ = bf16[8,16,512]{2,1,0:T(8,128)(2,1)S(1)} all-to-all(bf16[8,16,512]{2,1,0:T(8,128)(2,1)S(1)} %spread.1), channel_id=1, replica_groups=mesh['y'=4,'z'=8,'core'=2,'dp'=4] {'z'}, dimensions={0} | all-to-all | bytes 262144 | tf_op jit(solution)/shard_map/all_to_all | solution.py:230
  18.2 2.3 %collective-permute-start.3 = (bf16[8,16,512]{2,1,0:T(8,128)(2,1)S(1)}, bf16[8,16,512]{2,1,0:T(8,128)(2,1)S(1)}, u32[]{:S(2)}, u32[]{:S(2)}) collective-permute-start(bf16[8,16,512]{2,1,0:T(8,128)(2,1)S(1)} %all_to_all.10.refs_4_), channel_id=1, source_target_pairs={{0,4},{4,0},{1,5},{5,1},{2,6},{6,2},{3,7},{7,3},{8,12},{12,8},{9,1... | collective-permute-start | bytes 393224 | tf_op jit(solution)/shard_map/ppermute | solution.py:234
  21.1 2.8 %collective-permute-start.1 = (bf16[8,16,512]{2,1,0:T(8,128)(2,1)S(1)}, bf16[8,16,512]{2,1,0:T(8,128)(2,1)S(1)}, u32[]{:S(2)}, u32[]{:S(2)}) collective-permute-start(bf16[8,16,512]{2,1,0:T(8,128)(2,1)S(1)} %all_to_all.10.refs_4_), channel_id=1, source_target_pairs={{0,192},{64,128},{128,64},{192,0},{1,193},{65,129},{129,65},{193,1... | collective-permute-start | bytes 393224 | tf_op jit(solution)/shard_map/ppermute | solution.py:234
  24.0 0.0 collective-permute-start.2
  24.0 1.3 %collective-permute-start = (bf16[8,16,512]{2,1,0:T(8,128)(2,1)S(1)}, bf16[8,16,512]{2,1,0:T(8,128)(2,1)S(1)}, u32[]{:S(2)}, u32[]{:S(2)}) collective-permute-start(bf16[8,16,512]{2,1,0:T(8,128)(2,1)S(1)} %all_to_all.10.refs_4_), channel_id=1, source_target_pairs={{0,128},{64,192},{128,0},{192,64},{1,129},{65,193},{129,1},{193,65... | collective-permute-start | bytes 393224 | tf_op jit(solution)/shard_map/ppermute | solution.py:234
  25.3 0.0 collective-permute-done.3.refs_5_
  25.3 0.0 copy-done
  25.3 0.0 copy-done.1
  25.3 0.0 copy-done.2
  25.3 0.0 copy-done.3
  25.3 2.3 %shard_map.85.refs_6_ = f32[64,1,128]{2,1,0:T(1,128)S(1)} custom-call(s32[1,64]{1,0:T(1,128)S(1)} %bitcast.21, f32[10,1,512]{2,1,0:T(1,128)S(1)} %bitcast.17, bf16[9,512,512]{2,1,0:T(8,128)(2,1)S(1)} %bitcast.9, bf16[9,512,512]{2,1,0:T(8,128)(2,1)S(1)} %bitcast.13, bf16[8,16,512]{2,1,0:T(8,128)(2,1)S(1)} %all_to_all.10.refs_4_, ...), custom_call_target="tpu_custom_call" | custom-call | flops 1677721600 | bytes 1048576 | tf_op jit(solution)/shard_map/pallas_call | solution.py:163
  27.6 0.0 collective-permute-done.1.refs_4_
  27.6 1.1 %collective-permute-done.2.refs_5_ = bf16[8,16,512]{2,1,0:T(8,128)(2,1)S(1)} collective-permute-done((bf16[8,16,512]{2,1,0:T(8,128)(2,1)S(1)}, bf16[8,16,512]{2,1,0:T(8,128)(2,1)S(1)}, u32[]{:S(2)}, u32[]{:S(2)}) %collective-permute-start.2) | collective-permute-done | bytes 131104 | tf_op jit(solution)/shard_map/ppermute | solution.py:234
  28.7 1.9 %collective-permute-start.5 = (bf16[8,16,512]{2,1,0:T(8,128)(2,1)S(1)}, bf16[8,16,512]{2,1,0:T(8,128)(2,1)S(1)}, u32[]{:S(2)}, u32[]{:S(2)}) collective-permute-start(bf16[8,16,512]{2,1,0:T(8,128)(2,1)S(1)} %collective-permute-done.1.refs_4_), channel_id=1, source_target_pairs={{0,4},{4,0},{1,5},{5,1},{2,6},{6,2},{3,7},{7,3},{8,12},{12,8},{9,1... | collective-permute-start | bytes 393224 | tf_op jit(solution)/shard_map/ppermute | solution.py:234
  30.6 0.0 collective-permute-start.6
  30.6 2.3 %shard_map.86.refs_6_ = f32[64,1,128]{2,1,0:T(1,128)S(1)} custom-call(s32[1,64]{1,0:T(1,128)S(1)} %bitcast.22, f32[10,1,512]{2,1,0:T(1,128)S(1)} %bitcast.18, bf16[9,512,512]{2,1,0:T(8,128)(2,1)S(1)} %bitcast.10, bf16[9,512,512]{2,1,0:T(8,128)(2,1)S(1)} %bitcast.14, ...), custom_call_target="tpu_custom_call", output_to_operand_aliasing={{}: (6, {})} | custom-call | flops 1677721600 | bytes 1048576 | tf_op jit(solution)/shard_map/pallas_call | solution.py:163
  32.9 0.0 collective-permute-done.refs_4_
  32.9 0.5 %collective-permute-start.4 = (bf16[8,16,512]{2,1,0:T(8,128)(2,1)S(1)}, bf16[8,16,512]{2,1,0:T(8,128)(2,1)S(1)}, u32[]{:S(2)}, u32[]{:S(2)}) collective-permute-start(bf16[8,16,512]{2,1,0:T(8,128)(2,1)S(1)} %collective-permute-done.refs_4_), channel_id=1, source_target_pairs={{0,4},{4,0},{1,5},{5,1},{2,6},{6,2},{3,7},{7,3},{8,12},{12,8},{9,1... | collective-permute-start | bytes 393224 | tf_op jit(solution)/shard_map/ppermute | solution.py:234
  33.5 0.0 collective-permute-done.5.refs_4_
  33.5 0.0 collective-permute-done.6.refs_5_
  33.5 2.3 %shard_map.87.refs_6_ = f32[64,1,128]{2,1,0:T(1,128)S(1)} custom-call(s32[1,64]{1,0:T(1,128)S(1)} %bitcast.23, f32[10,1,512]{2,1,0:T(1,128)S(1)} %bitcast.19, bf16[9,512,512]{2,1,0:T(8,128)(2,1)S(1)} %bitcast.11, bf16[9,512,512]{2,1,0:T(8,128)(2,1)S(1)} %bitcast.15, ...), custom_call_target="tpu_custom_call", output_to_operand_aliasing={{}: (6, {})} | custom-call | flops 1677721600 | bytes 1048576 | tf_op jit(solution)/shard_map/pallas_call | solution.py:163
  35.8 0.0 collective-permute-done.4.refs_5_
  35.8 2.3 %shard_map.88 = f32[64,1,128]{2,1,0:T(1,128)S(1)} custom-call(s32[1,64]{1,0:T(1,128)S(1)} %bitcast.24, f32[10,1,512]{2,1,0:T(1,128)S(1)} %bitcast.20, bf16[9,512,512]{2,1,0:T(8,128)(2,1)S(1)} %bitcast.12, bf16[9,512,512]{2,1,0:T(8,128)(2,1)S(1)} %bitcast.16, bf16[8,16,512]{2,1,0:T(8,128)(2,1)S(1)} %collective-permute-done.refs_4_, ...), custom_call_target="tpu_custom_call", output_to_operand_aliasing={{}: (6, {})} | custom-call | flops 1677721600 | bytes 1048576 | tf_op jit(solution)/shard_map/pallas_call | solution.py:163
  38.1 12.9 %all_to_all.11.columns = f32[64,1,128]{2,1,0:T(1,128)S(1)} all-to-all(f32[64,1,128]{2,1,0:T(1,128)S(1)} %shard_map.88), channel_id=1, replica_groups=mesh['y'=4,'z'=8,'core'=2,'dp'=4] {'y','z','core'}, dimensions={0} | all-to-all | bytes 65536 | tf_op jit(solution)/shard_map/all_to_all | solution.py:230
  51.1 0.7 %statistics.1 = (f32[1,256]{1,0:T(1,128)}, f32[1,128]{1,0:T(1,128)}, f32[1,128]{1,0:T(1,128)}) custom-call(f32[64,1,128]{2,1,0:T(1,128)S(1)} %all_to_all.11.columns), custom_call_target="tpu_custom_call" | custom-call | tf_op jit(solution)/shard_map/statistics/pallas_call | solution.py:215
  (1 shorter events, 0.0 us)
Async XLA Ops:
  0.6 0.7 %copy-start.4 = (bf16[1,4,4,512]{3,2,1,0:T(4,128)(2,1)S(1)}, bf16[1,4,4,512]{3,2,1,0:T(4,128)(2,1)}, u32[]{:S(2)}) copy-start(bf16[1,4,4,512]{3,2,1,0:T(4,128)(2,1)} %param.6) | copy-start | bytes 49156
  1.4 23.9 %copy-start = (bf16[1,9,512,512]{3,2,1,0:T(8,128)(2,1)S(1)}, bf16[1,9,512,512]{3,2,1,0:T(8,128)(2,1)}, u32[]{:S(2)}) copy-start(bf16[1,9,512,512]{3,2,1,0:T(8,128)(2,1)} %param.9) | copy-start | bytes 14155780
  1.4 23.9 %copy-start.1 = (bf16[1,9,512,512]{3,2,1,0:T(8,128)(2,1)S(1)}, bf16[1,9,512,512]{3,2,1,0:T(8,128)(2,1)}, u32[]{:S(2)}) copy-start(bf16[1,9,512,512]{3,2,1,0:T(8,128)(2,1)} %param.10) | copy-start | bytes 14155780
  1.4 23.9 %copy-start.2 = (f32[1,512,10]{1,0,2:T(1,128)S(1)}, f32[1,512,10]{1,0,2:T(1,128)}, u32[]{:S(2)}) copy-start(f32[1,512,10]{1,0,2:T(1,128)} %param.11) | copy-start | bytes 61444
  1.4 23.9 %copy-start.3 = (s32[64]{0:T(128)S(1)}, s32[64]{0:T(128)}, u32[]{:S(2)}) copy-start(s32[64]{0:T(128)} %param.7) | copy-start | bytes 772
  18.2 7.1 %collective-permute-start.3 = (bf16[8,16,512]{2,1,0:T(8,128)(2,1)S(1)}, bf16[8,16,512]{2,1,0:T(8,128)(2,1)S(1)}, u32[]{:S(2)}, u32[]{:S(2)}) collective-permute-start(bf16[8,16,512]{2,1,0:T(8,128)(2,1)S(1)} %all_to_all.10.refs_4_), channel_id=1, source_target_pairs={{0,4},{4,0},{1,5},{5,1},{2,6},{6,2},{3,7},{7,3},{8,12},{12,8},{9,1... | collective-permute-start | bytes 393224 | tf_op jit(solution)/shard_map/ppermute | solution.py:234
  21.1 6.5 %collective-permute-start.1 = (bf16[8,16,512]{2,1,0:T(8,128)(2,1)S(1)}, bf16[8,16,512]{2,1,0:T(8,128)(2,1)S(1)}, u32[]{:S(2)}, u32[]{:S(2)}) collective-permute-start(bf16[8,16,512]{2,1,0:T(8,128)(2,1)S(1)} %all_to_all.10.refs_4_), channel_id=1, source_target_pairs={{0,192},{64,128},{128,64},{192,0},{1,193},{65,129},{129,65},{193,1... | collective-permute-start | bytes 393224 | tf_op jit(solution)/shard_map/ppermute | solution.py:234
  24.0 4.8 %collective-permute-start.2 = (bf16[8,16,512]{2,1,0:T(8,128)(2,1)S(1)}, bf16[8,16,512]{2,1,0:T(8,128)(2,1)S(1)}, u32[]{:S(2)}, u32[]{:S(2)}) collective-permute-start(bf16[8,16,512]{2,1,0:T(8,128)(2,1)S(1)} %all_to_all.10.refs_4_), channel_id=1, source_target_pairs={{0,64},{64,0},{128,192},{192,128},{1,65},{65,1},{129,193},{193,129... | collective-permute-start | bytes 393224 | tf_op jit(solution)/shard_map/ppermute | solution.py:234
  24.0 9.0 %collective-permute-start = (bf16[8,16,512]{2,1,0:T(8,128)(2,1)S(1)}, bf16[8,16,512]{2,1,0:T(8,128)(2,1)S(1)}, u32[]{:S(2)}, u32[]{:S(2)}) collective-permute-start(bf16[8,16,512]{2,1,0:T(8,128)(2,1)S(1)} %all_to_all.10.refs_4_), channel_id=1, source_target_pairs={{0,128},{64,192},{128,0},{192,64},{1,129},{65,193},{129,1},{193,65... | collective-permute-start | bytes 393224 | tf_op jit(solution)/shard_map/ppermute | solution.py:234
  28.7 4.7 %collective-permute-start.5 = (bf16[8,16,512]{2,1,0:T(8,128)(2,1)S(1)}, bf16[8,16,512]{2,1,0:T(8,128)(2,1)S(1)}, u32[]{:S(2)}, u32[]{:S(2)}) collective-permute-start(bf16[8,16,512]{2,1,0:T(8,128)(2,1)S(1)} %collective-permute-done.1.refs_4_), channel_id=1, source_target_pairs={{0,4},{4,0},{1,5},{5,1},{2,6},{6,2},{3,7},{7,3},{8,12},{12,8},{9,1... | collective-permute-start | bytes 393224 | tf_op jit(solution)/shard_map/ppermute | solution.py:234
  30.6 2.9 %collective-permute-start.6 = (bf16[8,16,512]{2,1,0:T(8,128)(2,1)S(1)}, bf16[8,16,512]{2,1,0:T(8,128)(2,1)S(1)}, u32[]{:S(2)}, u32[]{:S(2)}) collective-permute-start(bf16[8,16,512]{2,1,0:T(8,128)(2,1)S(1)} %collective-permute-done.2.refs_5_), channel_id=1, source_target_pairs={{0,4},{4,0},{1,5},{5,1},{2,6},{6,2},{3,7},{7,3},{8,12},{12,8},{9,1... | collective-permute-start | bytes 393224 | tf_op jit(solution)/shard_map/ppermute | solution.py:234
  32.9 2.9 %collective-permute-start.4 = (bf16[8,16,512]{2,1,0:T(8,128)(2,1)S(1)}, bf16[8,16,512]{2,1,0:T(8,128)(2,1)S(1)}, u32[]{:S(2)}, u32[]{:S(2)}) collective-permute-start(bf16[8,16,512]{2,1,0:T(8,128)(2,1)S(1)} %collective-permute-done.refs_4_), channel_id=1, source_target_pairs={{0,4},{4,0},{1,5},{5,1},{2,6},{6,2},{3,7},{7,3},{8,12},{12,8},{9,1... | collective-permute-start | bytes 393224 | tf_op jit(solution)/shard_map/ppermute | solution.py:234
where the time goes:
time: 52.1 us; the launch traced here: 51.8 us
  blocking collectives  29.8 us (57%)
  Pallas kernels  9.99 us (19%)
  starting transfers between devices  8.82 us (17%)
  between operations  1.34 us (3%)
  waiting for transfers between devices  1.16 us (2%)
  local copies, waits for them, and re-layouts  0.73 us (1%)
    all_to_all x2, blocking collectives, exchanged(): return lax.all_to_all(x, axis, 0, 0, tiled=True)  29.8 us
    pallas_call x4, Pallas kernels, conv_call(): pl.pallas_call(functools.partial(conv_kernel, columns), out_shape=pltpu.V...  9.26 us
    ppermute x7, starting transfers between devices, swapped(): lax.ppermute(x, axis, [(i, i ^ mask) for i in range(lax.axis_size(axis))])  8.82 us
    ppermute x7, waiting for transfers between devices, swapped(): lax.ppermute(x, axis, [(i, i ^ mask) for i in range(lax.axis_size(axis))])  1.16 us
  transfers between devices with their start and end apart: 7, of which 1 were waited for; matrix products, arithmetic and copies ran while one was open for 0% of the time, Pallas kernels for 13%

commit v1 on v0

--- a/solution.py
+++ b/solution.py
@@ -68,16 +68,60 @@
             moved[:, pl.ds(g * GROUP, GROUP), pl.ds(n * HALF, HALF)] = got.reshape(SPOTS, GROUP, HALF)
 
 
-def conv_kernel(columns, *refs):
-    labels, head, w1, w2 = refs[:4]
-    grids = refs[4 : 4 + len(columns)]
-    ident = refs[5 + len(columns)] if len(refs) == 10 + len(columns) else None
-    out, moved, hidden, pooled = refs[-4:]
+def margins_of(pooled, label, head):
+    wide = (pooled.shape[0], 128)
+    lane = lax.broadcasted_iota(jnp.int32, wide, 1)
+    logits = jnp.full(wide, -1e30, jnp.float32)
+    for k in range(CLASSES):
+        total = pooled[:, :128] * head[k, :, pl.ds(0, 128)]
+        for j in range(1, 4):
+            total = total + pooled[:, j * 128 : j * 128 + 128] * head[k, :, pl.ds(j * 128, 128)]
+        logits = jnp.where(lane == k, jnp.sum(total, axis=1, keepdims=True), logits)
+    chosen = lane == label
+    correct = jnp.sum(jnp.where(chosen, logits, 0.0), axis=1, keepdims=True)
+    rival = jnp.max(jnp.where(chosen, -1e30, logits), axis=1, keepdims=True)
+    return correct - rival
+
+
+def conv_kernel(columns, step, last, *refs):
+    refs = list(refs)
+    w1, w2, *grids = refs[: 2 + len(columns[step])]
+    refs = refs[2 + len(columns[step]) :]
+    if step:
+        before = refs.pop(0)
+    if last:
+        labels, head, ident, out = refs[:4]
+    else:
+        store = refs[0]
+    moved, hidden = refs[-2:]
     targets = moved.shape[1]
     deep = grids[0].shape[0]
     groups = targets // GROUP
     sources = [grids[2 * g : 2 * g + 2] for g in range(groups)]
 
+    if last:
+        core, y = lax.axis_index("core"), lax.axis_index("y")
+        wide = (targets, 128)
+        lane = lax.broadcasted_iota(jnp.int32, wide, 1)
+        line = lax.broadcasted_iota(jnp.int32, wide, 0)
+        few = labels.shape[1]
+        spread_labels = jnp.broadcast_to(labels[...].astype(jnp.float32), (targets, few))
+
+        def send(part, pooled):
+            firsts = []
+            for mask, swap in columns[part]:
+                first = lax.bitwise_xor(y, jnp.int32(mask)) * (2 * deep)
+                firsts.append(first + (1 - core if swap else core))
+            place = 2 * (line & (deep - 1))
+            for i, first in enumerate(firsts):
+                place = place + jnp.where(line // deep == i, first, 0)
+            mine = jnp.where(place[:, :few] == lane[:, :few], spread_labels, 0.0)
+            label = jnp.sum(mine, axis=1, keepdims=True).astype(jnp.int32)
+            margin = margins_of(pooled, label, head)
+            packed = jnp.where(lane < 64, margin, ident[0].astype(jnp.float32))
+            for i in range(targets):
+                out[pl.ds(firsts[i // deep] + 2 * (i % deep), 1), 0, :] = packed[i : i + 1, :]
+
     def shuffle(*flat):
         by_position(sources, moved, (flat[:groups], flat[groups:]))
 
@@ -85,6 +129,9 @@
         shuffle,
         *[pltpu.ACC(n)((HALF, HALF), jnp.float32) for n in range(2) for _ in range(groups)],
     )
+    if last:
+        for part in range(step):
+            send(part, before[pl.ds(part * targets, targets), :])
 
     def both(*flat):
         accs = (flat[:SPOTS], flat[SPOTS:])
@@ -94,81 +141,53 @@
                 got = jnp.maximum(pltpu.matmul_pop(accs[n][spot]), 0.0)
                 hidden[spot, :, pl.ds(n * HALF, HALF)] = got.astype(jnp.bfloat16)
         convolve(hidden, w2, accs)
+        best = [None, None]
         for spot in range(SPOTS):
             for n in range(2):
-                cols = pl.ds(n * HALF, HALF)
                 got = jnp.maximum(pltpu.matmul_pop(accs[n][spot]), 0.0)
-                got = got + moved[spot, :, cols].astype(jnp.float32)
-                if spot:
-                    got = jnp.maximum(got, pooled[:, cols])
-                pooled[:, cols] = got
+                got = got + moved[spot, :, pl.ds(n * HALF, HALF)].astype(jnp.float32)
+                best[n] = jnp.maximum(best[n], got) if spot else got
+        pooled = jnp.concatenate(best, axis=1)
+        if last:
+            send(step, pooled)
+        else:
+            store[pl.ds(step * targets, targets), :] = pooled
 
     pl.run_scoped(
         both,
         *[pltpu.ACC(n)((targets, HALF), jnp.float32) for n in range(2) for _ in range(SPOTS)],
     )
 
-    core, y = lax.axis_index("core"), lax.axis_index("y")
-    firsts = []
-    for mask, swap in columns:
-        first = lax.bitwise_xor(y, jnp.int32(mask)) * (2 * deep)
-        firsts.append(first + (1 - core if swap else core))
-    wide = (targets, 128)
-    lane = lax.broadcasted_iota(jnp.int32, wide, 1)
-    line = lax.broadcasted_iota(jnp.int32, wide, 0)
-    place = 2 * (line & (deep - 1))
-    for i, first in enumerate(firsts):
-        place = place + jnp.where(line // deep == i, first, 0)
-    few = labels.shape[1]
-    spread_labels = jnp.broadcast_to(labels[...].astype(jnp.float32), (targets, few))
-    mine = jnp.where(place[:, :few] == lane[:, :few], spread_labels, 0.0)
-    label = jnp.sum(mine, axis=1, keepdims=True).astype(jnp.int32)
-    logits = jnp.full(wide, -1e30, jnp.float32)
-    for k in range(CLASSES):
-        total = pooled[:, pl.ds(0, 128)] * head[k, :, pl.ds(0, 128)]
-        for j in range(1, 4):
-            cols = pl.ds(j * 128, 128)
-            total = total + pooled[:, cols] * head[k, :, cols]
-        logits = jnp.where(lane == k, jnp.sum(total, axis=1, keepdims=True), logits)
-    chosen = lane == label
-    correct = jnp.sum(jnp.where(chosen, logits, 0.0), axis=1, keepdims=True)
-    rival = jnp.max(jnp.where(chosen, -1e30, logits), axis=1, keepdims=True)
-    packed = jnp.broadcast_to(correct - rival, wide)
-    for i in range(targets):
-        out[pl.ds(firsts[i // deep] + 2 * (i % deep), 1), 0, :] = packed[i : i + 1, :]
-    if ident is not None:
-        whole = out[...]
-        low = lax.broadcasted_iota(jnp.int32, whole.shape, 2) < 64
-        out[...] = jnp.where(low, whole, ident[0].astype(jnp.float32))
-
 
 def in_vmem(x):
     return pltpu.with_memory_space_constraint(x, pltpu.VMEM)
 
 
-def conv_call(columns, grids, labels, head, w1, w2, before=None, ident=None):
+def conv_call(columns, step, grids, w1, w2, before=None, tail=None):
     targets = sum(grid.shape[0] for grid in grids)
     vmem = pl.BlockSpec(memory_space=pltpu.VMEM)
-    operands = [labels, head, *map(in_vmem, (w1, w2, *grids))]
-    specs = [vmem] * len(operands)
+    operands = [*map(in_vmem, (w1, w2, *grids))]
     aliases = {}
     if before is not None:
-        aliases = {len(operands): 0}
+        if tail is None:
+            aliases = {len(operands): 0}
         operands.append(in_vmem(before))
-        specs.append(vmem)
-    if ident is not None:
-        operands.append(ident)
-        specs.append(pl.BlockSpec(memory_space=pltpu.SMEM))
+    specs = [vmem] * len(operands)
+    if tail is None:
+        out_shape = pltpu.VMEM((targets * len(columns), 512), jnp.float32)
+    else:
+        operands += tail
+        specs += [vmem, vmem, pl.BlockSpec(memory_space=pltpu.SMEM)]
+        out_shape = pltpu.VMEM((targets * len(columns), 1, 128), jnp.float32)
     work = 2 * 100 * targets * 512 * 512 * 2
     return pl.pallas_call(
-        functools.partial(conv_kernel, columns),
-        out_shape=pltpu.VMEM((64, 1, 128), jnp.float32),
+        functools.partial(conv_kernel, columns, step, tail is not None),
+        out_shape=out_shape,
         in_specs=specs,
         out_specs=vmem,
         scratch_shapes=[
             pltpu.VMEM((SPOTS, targets, 512), jnp.bfloat16),
             pltpu.VMEM((SPOTS, targets, 512), jnp.bfloat16),
-            pltpu.VMEM((targets, 512), jnp.float32),
         ],
         input_output_aliases=aliases,
         cost_estimate=pl.CostEstimate(flops=work, bytes_accessed=1 << 20, transcendentals=0),
@@ -237,20 +256,26 @@
 def staged(features, labels, subset_ids, conv1_weight, conv2_weight, head_weight):
     column = exchanged(spread_call(features[0], lax.axis_size("z")), "z")
     head = jnp.transpose(head_weight, (2, 0, 1))
-    fixed = (labels.reshape(1, -1), head, conv1_weight[0], conv2_weight[0])
+    fixed = (conv1_weight[0], conv2_weight[0])
     column_o = swapped(column, "core", 1)
-    near = swapped(column, "y", 3)
-    next_ = swapped(column, "y", 1)
+    near = swapped(column, "y", 1)
+    next_ = swapped(column, "y", 3)
     far = swapped(column, "y", 2)
-    packed = conv_call(((0, False), (0, True)), (column, column_o), *fixed)
-    near, next_, packed = lax.optimization_barrier((near, next_, packed))
+    plan = (
+        ((0, False), (0, True)),
+        ((1, False), (3, False)),
+        ((1, True), (3, True)),
+        ((2, False), (2, True)),
+    )
+    pooled = conv_call(plan, 0, (column, column_o), *fixed)
+    near, next_, pooled = lax.optimization_barrier((near, next_, pooled))
     near_o, next_o = swapped(near, "core", 1), swapped(next_, "core", 1)
-    packed = conv_call(((3, False), (1, False)), (near, next_), *fixed, packed)
-    far, packed = lax.optimization_barrier((far, packed))
+    pooled = conv_call(plan, 1, (near, next_), *fixed, pooled)
+    far, pooled = lax.optimization_barrier((far, pooled))
     far_o = swapped(far, "core", 1)
-    packed = conv_call(((3, True), (1, True)), (near_o, next_o), *fixed, packed)
-    ident, packed = lax.optimization_barrier((subset_ids, packed))
-    packed = conv_call(((2, False), (2, True)), (far, far_o), *fixed, packed, ident)
+    pooled = conv_call(plan, 2, (near_o, next_o), *fixed, pooled)
+    tail = (labels.reshape(1, -1), head, subset_ids)
+    packed = conv_call(plan, 3, (far, far_o), *fixed, pooled, tail)
     columns = exchanged(packed, ("y", "z", "core"))
     datamodel, mean, norm = tail_call(columns)
     return (datamodel, mean[0, :1], norm[0, :1])

time: 52.1 us -> 53.9 us (1.035)
  blocking collectives: 29.8 us -> 31.6 us
  waiting for transfers between devices: 1.16 us -> 2.37 us
  starting transfers between devices: 8.82 us -> 8.2 us
  Pallas kernels: 9.99 us -> 9.44 us
    all_to_all x2, blocking collectives: 29.8 us -> 31.6 us  [exchanged(): return lax.all_to_all(x, axis, 0, 0, tiled=True)]
    ppermute x7, waiting for transfers between devices: 1.16 us -> 2.37 us  [swapped(): lax.ppermute(x, axis, [(i, i ^ mask) for i in range(lax.axis_size(axis))])]
    ppermute x7, starting transfers between devices: 8.82 us -> 8.2 us  [swapped(): lax.ppermute(x, axis, [(i, i ^ mask) for i in range(lax.axis_size(axis))])]
    pallas_call x4, Pallas kernels: 9.26 us -> 8.71 us  [conv_call(): pl.pallas_call(functools.partial(conv_kernel, columns, step, tail is not...]
  transfers between devices with their start and end apart: 7 -> 7, of which waited for: 1 -> 1; matrix products, arithmetic and copies ran while one was open for 0% -> 0% of each run, Pallas kernels for 13% -> 12%
where the time goes in v1:
time: 53.9 us; the launch traced here: 53.7 us
  blocking collectives  31.6 us (59%)
  Pallas kernels  9.44 us (18%)
  starting transfers between devices  8.2 us (15%)
  waiting for transfers between devices  2.37 us (4%)
  between operations  1.38 us (3%)
  local copies, waits for them, and re-layouts  0.73 us (1%)
    all_to_all x2, blocking collectives, exchanged(): return lax.all_to_all(x, axis, 0, 0, tiled=True)  31.6 us
    pallas_call x4, Pallas kernels, conv_call(): pl.pallas_call(functools.partial(conv_kernel, columns, step, tail is not...  8.71 us
    ppermute x7, starting transfers between devices, swapped(): lax.ppermute(x, axis, [(i, i ^ mask) for i in range(lax.axis_size(axis))])  8.2 us
    ppermute x7, waiting for transfers between devices, swapped(): lax.ppermute(x, axis, [(i, i ^ mask) for i in range(lax.axis_size(axis))])  2.37 us
  transfers between devices with their start and end apart: 7, of which 1 were waited for; matrix products, arithmetic and copies ran while one was open for 0% of the time, Pallas kernels for 12%

profile of v1, /device:TPU:1, one launch (start us, length us, event | category | flops | bytes accessed | tf_op | source)
XLA Modules:
  0.0 53.7 jit_solution(8039579428070157199)
XLA Ops:
  0.6 0.0 copy-start.4
  0.6 0.7 %copy-done.4 = bf16[1,4,4,512]{3,2,1,0:T(4,128)(2,1)S(1)} copy-done((bf16[1,4,4,512]{3,2,1,0:T(4,128)(2,1)S(1)}, bf16[1,4,4,512]{3,2,1,0:T(4,128)(2,1)}, u32[]{:S(2)}) %copy-start.4) | copy-done | bytes 16408
  1.3 0.0 copy-start
  1.4 0.0 copy-start.1
  1.4 16.8 %all_to_all.10.refs_2_ = bf16[8,16,512]{2,1,0:T(8,128)(2,1)S(1)} all-to-all(bf16[8,16,512]{2,1,0:T(8,128)(2,1)S(1)} %spread.1), channel_id=1, replica_groups=mesh['y'=4,'z'=8,'core'=2,'dp'=4] {'z'}, dimensions={0} | all-to-all | bytes 262144 | tf_op jit(solution)/shard_map/all_to_all | solution.py:249
  18.2 2.3 %collective-permute-start.3 = (bf16[8,16,512]{2,1,0:T(8,128)(2,1)S(1)}, bf16[8,16,512]{2,1,0:T(8,128)(2,1)S(1)}, u32[]{:S(2)}, u32[]{:S(2)}) collective-permute-start(bf16[8,16,512]{2,1,0:T(8,128)(2,1)S(1)} %all_to_all.10.refs_2_), channel_id=1, source_target_pairs={{0,4},{4,0},{1,5},{5,1},{2,6},{6,2},{3,7},{7,3},{8,12},{12,8},{9,1... | collective-permute-start | bytes 393224 | tf_op jit(solution)/shard_map/ppermute | solution.py:253
  21.1 1.4 %collective-permute-start.1 = (bf16[8,16,512]{2,1,0:T(8,128)(2,1)S(1)}, bf16[8,16,512]{2,1,0:T(8,128)(2,1)S(1)}, u32[]{:S(2)}, u32[]{:S(2)}) collective-permute-start(bf16[8,16,512]{2,1,0:T(8,128)(2,1)S(1)} %all_to_all.10.refs_2_), channel_id=1, source_target_pairs={{0,64},{64,0},{128,192},{192,128},{1,65},{65,1},{129,193},{193,129... | collective-permute-start | bytes 393224 | tf_op jit(solution)/shard_map/ppermute | solution.py:253
  22.5 1.9 %collective-permute-start.2 = (bf16[8,16,512]{2,1,0:T(8,128)(2,1)S(1)}, bf16[8,16,512]{2,1,0:T(8,128)(2,1)S(1)}, u32[]{:S(2)}, u32[]{:S(2)}) collective-permute-start(bf16[8,16,512]{2,1,0:T(8,128)(2,1)S(1)} %all_to_all.10.refs_2_), channel_id=1, source_target_pairs={{0,192},{64,128},{128,64},{192,0},{1,193},{65,129},{129,65},{193,1... | collective-permute-start | bytes 393224 | tf_op jit(solution)/shard_map/ppermute | solution.py:253
  24.4 0.7 %collective-permute-start = (bf16[8,16,512]{2,1,0:T(8,128)(2,1)S(1)}, bf16[8,16,512]{2,1,0:T(8,128)(2,1)S(1)}, u32[]{:S(2)}, u32[]{:S(2)}) collective-permute-start(bf16[8,16,512]{2,1,0:T(8,128)(2,1)S(1)} %all_to_all.10.refs_2_), channel_id=1, source_target_pairs={{0,128},{64,192},{128,0},{192,64},{1,129},{65,193},{129,1},{193,65... | collective-permute-start | bytes 393224 | tf_op jit(solution)/shard_map/ppermute | solution.py:253
  25.1 0.0 collective-permute-done.3.refs_3_
  25.1 0.0 copy-done
  25.1 0.0 copy-done.1
  25.2 2.1 %shard_map.85.refs_4_ = f32[64,512]{1,0:T(8,128)S(1)} custom-call(bf16[9,512,512]{2,1,0:T(8,128)(2,1)S(1)} %bitcast.9, bf16[9,512,512]{2,1,0:T(8,128)(2,1)S(1)} %bitcast.13, bf16[8,16,512]{2,1,0:T(8,128)(2,1)S(1)} %all_to_all.10.refs_2_, bf16[8,16,512]{2,1,0:T(8,128)(2,1)S(1)} %collective-permute-done.3.refs_3_), custom_call_target="tpu_custom_call" | custom-call | flops 1677721600 | bytes 1048576 | tf_op jit(solution)/shard_map/pallas_call | solution.py:183
  27.3 0.0 collective-permute-done.1.refs_2_
  27.3 2.4 %collective-permute-done.2.refs_3_ = bf16[8,16,512]{2,1,0:T(8,128)(2,1)S(1)} collective-permute-done((bf16[8,16,512]{2,1,0:T(8,128)(2,1)S(1)}, bf16[8,16,512]{2,1,0:T(8,128)(2,1)S(1)}, u32[]{:S(2)}, u32[]{:S(2)}) %collective-permute-start.2) | collective-permute-done | bytes 131104 | tf_op jit(solution)/shard_map/ppermute | solution.py:253
  29.7 1.3 %collective-permute-start.5 = (bf16[8,16,512]{2,1,0:T(8,128)(2,1)S(1)}, bf16[8,16,512]{2,1,0:T(8,128)(2,1)S(1)}, u32[]{:S(2)}, u32[]{:S(2)}) collective-permute-start(bf16[8,16,512]{2,1,0:T(8,128)(2,1)S(1)} %collective-permute-done.1.refs_2_), channel_id=1, source_target_pairs={{0,4},{4,0},{1,5},{5,1},{2,6},{6,2},{3,7},{7,3},{8,12},{12,8},{9,1... | collective-permute-start | bytes 393224 | tf_op jit(solution)/shard_map/ppermute | solution.py:253
  30.9 0.0 collective-permute-start.6
  30.9 2.1 %shard_map.86.refs_4_ = f32[64,512]{1,0:T(8,128)S(1)} custom-call(bf16[9,512,512]{2,1,0:T(8,128)(2,1)S(1)} %bitcast.10, bf16[9,512,512]{2,1,0:T(8,128)(2,1)S(1)} %bitcast.14, bf16[8,16,512]{2,1,0:T(8,128)(2,1)S(1)} %collective-permute-done.1.refs_2_, bf16[8,16,512]{2,1,0:T(8,128)(2,1)S(1)} %collective-permute-done.2.refs_3_, ...), custom_call_target="tpu_custom_call", output_to_operand_aliasing={{}: (4, {})} | custom-call | flops 1677721600 | bytes 1048576 | tf_op jit(solution)/shard_map/pallas_call | solution.py:183
  33.1 0.0 copy-start.2
  33.1 0.0 copy-start.3
  33.1 0.0 collective-permute-done.refs_2_
  33.1 0.6 %collective-permute-start.4 = (bf16[8,16,512]{2,1,0:T(8,128)(2,1)S(1)}, bf16[8,16,512]{2,1,0:T(8,128)(2,1)S(1)}, u32[]{:S(2)}, u32[]{:S(2)}) collective-permute-start(bf16[8,16,512]{2,1,0:T(8,128)(2,1)S(1)} %collective-permute-done.refs_2_), channel_id=1, source_target_pairs={{0,4},{4,0},{1,5},{5,1},{2,6},{6,2},{3,7},{7,3},{8,12},{12,8},{9,1... | collective-permute-start | bytes 393224 | tf_op jit(solution)/shard_map/ppermute | solution.py:253
  33.7 0.0 collective-permute-done.5.refs_2_
  33.7 0.0 collective-permute-done.6.refs_3_
  33.7 2.1 %shard_map.87.refs_4_ = f32[64,512]{1,0:T(8,128)S(1)} custom-call(bf16[9,512,512]{2,1,0:T(8,128)(2,1)S(1)} %bitcast.11, bf16[9,512,512]{2,1,0:T(8,128)(2,1)S(1)} %bitcast.15, bf16[8,16,512]{2,1,0:T(8,128)(2,1)S(1)} %collective-permute-done.5.refs_2_, bf16[8,16,512]{2,1,0:T(8,128)(2,1)S(1)} %collective-permute-done.6.refs_3_, ...), custom_call_target="tpu_custom_call", output_to_operand_aliasing={{}: (4, {})} | custom-call | flops 1677721600 | bytes 1048576 | tf_op jit(solution)/shard_map/pallas_call | solution.py:183
  35.9 0.0 collective-permute-done.4.refs_3_
  35.9 0.0 copy-done.2
  35.9 0.0 copy-done.3
  35.9 2.3 %shard_map.88 = f32[64,1,128]{2,1,0:T(1,128)S(1)} custom-call(bf16[9,512,512]{2,1,0:T(8,128)(2,1)S(1)} %bitcast.12, bf16[9,512,512]{2,1,0:T(8,128)(2,1)S(1)} %bitcast.16, bf16[8,16,512]{2,1,0:T(8,128)(2,1)S(1)} %collective-permute-done.refs_2_, bf16[8,16,512]{2,1,0:T(8,128)(2,1)S(1)} %collective-permute-done.4.refs_3_, f32[64,512]{1,0:T(8,128)S(1)} %shard_map.87.refs_4_, ...), custom_call_target="tpu_custom_call" | custom-call | flops 1677721600 | bytes 1048576 | tf_op jit(solution)/shard_map/pallas_call | solution.py:183
  38.2 14.7 %all_to_all.11.columns = f32[64,1,128]{2,1,0:T(1,128)S(1)} all-to-all(f32[64,1,128]{2,1,0:T(1,128)S(1)} %shard_map.88), channel_id=1, replica_groups=mesh['y'=4,'z'=8,'core'=2,'dp'=4] {'y','z','core'}, dimensions={0} | all-to-all | bytes 65536 | tf_op jit(solution)/shard_map/all_to_all | solution.py:249
  53.0 0.7 %statistics.1 = (f32[1,256]{1,0:T(1,128)}, f32[1,128]{1,0:T(1,128)}, f32[1,128]{1,0:T(1,128)}) custom-call(f32[64,1,128]{2,1,0:T(1,128)S(1)} %all_to_all.11.columns), custom_call_target="tpu_custom_call" | custom-call | tf_op jit(solution)/shard_map/statistics/pallas_call | solution.py:234
  (1 shorter events, 0.0 us)
Async XLA Ops:
  0.6 0.7 %copy-start.4 = (bf16[1,4,4,512]{3,2,1,0:T(4,128)(2,1)S(1)}, bf16[1,4,4,512]{3,2,1,0:T(4,128)(2,1)}, u32[]{:S(2)}) copy-start(bf16[1,4,4,512]{3,2,1,0:T(4,128)(2,1)} %param.6) | copy-start | bytes 49156
  1.3 23.8 %copy-start = (bf16[1,9,512,512]{3,2,1,0:T(8,128)(2,1)S(1)}, bf16[1,9,512,512]{3,2,1,0:T(8,128)(2,1)}, u32[]{:S(2)}) copy-start(bf16[1,9,512,512]{3,2,1,0:T(8,128)(2,1)} %param.9) | copy-start | bytes 14155780
  1.4 23.8 %copy-start.1 = (bf16[1,9,512,512]{3,2,1,0:T(8,128)(2,1)S(1)}, bf16[1,9,512,512]{3,2,1,0:T(8,128)(2,1)}, u32[]{:S(2)}) copy-start(bf16[1,9,512,512]{3,2,1,0:T(8,128)(2,1)} %param.10) | copy-start | bytes 14155780
  18.2 7.0 %collective-permute-start.3 = (bf16[8,16,512]{2,1,0:T(8,128)(2,1)S(1)}, bf16[8,16,512]{2,1,0:T(8,128)(2,1)S(1)}, u32[]{:S(2)}, u32[]{:S(2)}) collective-permute-start(bf16[8,16,512]{2,1,0:T(8,128)(2,1)S(1)} %all_to_all.10.refs_2_), channel_id=1, source_target_pairs={{0,4},{4,0},{1,5},{5,1},{2,6},{6,2},{3,7},{7,3},{8,12},{12,8},{9,1... | collective-permute-start | bytes 393224 | tf_op jit(solution)/shard_map/ppermute | solution.py:253
  21.1 6.2 %collective-permute-start.1 = (bf16[8,16,512]{2,1,0:T(8,128)(2,1)S(1)}, bf16[8,16,512]{2,1,0:T(8,128)(2,1)S(1)}, u32[]{:S(2)}, u32[]{:S(2)}) collective-permute-start(bf16[8,16,512]{2,1,0:T(8,128)(2,1)S(1)} %all_to_all.10.refs_2_), channel_id=1, source_target_pairs={{0,64},{64,0},{128,192},{192,128},{1,65},{65,1},{129,193},{193,129... | collective-permute-start | bytes 393224 | tf_op jit(solution)/shard_map/ppermute | solution.py:253
  22.5 7.1 %collective-permute-start.2 = (bf16[8,16,512]{2,1,0:T(8,128)(2,1)S(1)}, bf16[8,16,512]{2,1,0:T(8,128)(2,1)S(1)}, u32[]{:S(2)}, u32[]{:S(2)}) collective-permute-start(bf16[8,16,512]{2,1,0:T(8,128)(2,1)S(1)} %all_to_all.10.refs_2_), channel_id=1, source_target_pairs={{0,192},{64,128},{128,64},{192,0},{1,193},{65,129},{129,65},{193,1... | collective-permute-start | bytes 393224 | tf_op jit(solution)/shard_map/ppermute | solution.py:253
  24.4 8.7 %collective-permute-start = (bf16[8,16,512]{2,1,0:T(8,128)(2,1)S(1)}, bf16[8,16,512]{2,1,0:T(8,128)(2,1)S(1)}, u32[]{:S(2)}, u32[]{:S(2)}) collective-permute-start(bf16[8,16,512]{2,1,0:T(8,128)(2,1)S(1)} %all_to_all.10.refs_2_), channel_id=1, source_target_pairs={{0,128},{64,192},{128,0},{192,64},{1,129},{65,193},{129,1},{193,65... | collective-permute-start | bytes 393224 | tf_op jit(solution)/shard_map/ppermute | solution.py:253
  29.7 4.1 %collective-permute-start.5 = (bf16[8,16,512]{2,1,0:T(8,128)(2,1)S(1)}, bf16[8,16,512]{2,1,0:T(8,128)(2,1)S(1)}, u32[]{:S(2)}, u32[]{:S(2)}) collective-permute-start(bf16[8,16,512]{2,1,0:T(8,128)(2,1)S(1)} %collective-permute-done.1.refs_2_), channel_id=1, source_target_pairs={{0,4},{4,0},{1,5},{5,1},{2,6},{6,2},{3,7},{7,3},{8,12},{12,8},{9,1... | collective-permute-start | bytes 393224 | tf_op jit(solution)/shard_map/ppermute | solution.py:253
  30.9 2.8 %collective-permute-start.6 = (bf16[8,16,512]{2,1,0:T(8,128)(2,1)S(1)}, bf16[8,16,512]{2,1,0:T(8,128)(2,1)S(1)}, u32[]{:S(2)}, u32[]{:S(2)}) collective-permute-start(bf16[8,16,512]{2,1,0:T(8,128)(2,1)S(1)} %collective-permute-done.2.refs_3_), channel_id=1, source_target_pairs={{0,4},{4,0},{1,5},{5,1},{2,6},{6,2},{3,7},{7,3},{8,12},{12,8},{9,1... | collective-permute-start | bytes 393224 | tf_op jit(solution)/shard_map/ppermute | solution.py:253
  33.1 2.8 %copy-start.2 = (f32[1,512,10]{1,0,2:T(1,128)S(1)}, f32[1,512,10]{1,0,2:T(1,128)}, u32[]{:S(2)}) copy-start(f32[1,512,10]{1,0,2:T(1,128)} %param.11) | copy-start | bytes 61444
  33.1 2.8 %copy-start.3 = (s32[64]{0:T(128)S(1)}, s32[64]{0:T(128)}, u32[]{:S(2)}) copy-start(s32[64]{0:T(128)} %param.7) | copy-start | bytes 772
  33.1 2.8 %collective-permute-start.4 = (bf16[8,16,512]{2,1,0:T(8,128)(2,1)S(1)}, bf16[8,16,512]{2,1,0:T(8,128)(2,1)S(1)}, u32[]{:S(2)}, u32[]{:S(2)}) collective-permute-start(bf16[8,16,512]{2,1,0:T(8,128)(2,1)S(1)} %collective-permute-done.refs_2_), channel_id=1, source_target_pairs={{0,4},{4,0},{1,5},{5,1},{2,6},{6,2},{3,7},{7,3},{8,12},{12,8},{9,1... | collective-permute-start | bytes 393224 | tf_op jit(solution)/shard_map/ppermute | solution.py:253

commit v2 on v1

--- a/solution.py
+++ b/solution.py
@@ -47,39 +47,31 @@
             stage = 1 - stage
 
 
-def by_position(sources, moved, accs):
-    lane = lax.broadcasted_iota(jnp.int32, (GROUP, HALF), 1)
-    target = lax.broadcasted_iota(jnp.int32, (GROUP, HALF), 0)
-    picks = [
-        jnp.where(lane == target * SPOTS + spot, 1.0, 0.0).astype(jnp.bfloat16)
-        for spot in range(SPOTS)
-    ]
-    pick = jnp.concatenate(picks, axis=0)
+def by_position(sources, moved, wide):
     for g, refs in enumerate(sources):
-        for n in range(2):
-            block = [ref[:, :, pl.ds(n * HALF, HALF)].reshape(-1, HALF) for ref in refs]
-            pltpu.matmul_push_rhs(
-                jnp.concatenate(block, axis=0), staging_register=g % 2, mxu_index=n
-            )
-            pltpu.matmul_acc_lhs(accs[n][g], pick, load_staged_rhs=g % 2)
-    for g in range(len(sources)):
-        for n in range(2):
-            got = pltpu.matmul_pop(accs[n][g]).astype(jnp.bfloat16)
-            moved[:, pl.ds(g * GROUP, GROUP), pl.ds(n * HALF, HALF)] = got.reshape(SPOTS, GROUP, HALF)
+        at = 0
+        for ref in refs:
+            rows = ref.shape[0] * SPOTS
+            for j in range(wide.shape[0]):
+                part = ref[:, :, pl.ds(j * 128, 128)].reshape(rows, 128)
+                wide[j, pl.ds(at, rows), :] = part.astype(jnp.float32)
+            at += rows
+        for spot in range(SPOTS):
+            for j in range(wide.shape[0]):
+                picked = wide[j, pl.ds(spot, GROUP, stride=SPOTS), :]
+                moved[spot, pl.ds(g * GROUP, GROUP), pl.ds(j * 128, 128)] = picked.astype(jnp.bfloat16)
 
 
 def margins_of(pooled, label, head):
-    wide = (pooled.shape[0], 128)
-    lane = lax.broadcasted_iota(jnp.int32, wide, 1)
-    logits = jnp.full(wide, -1e30, jnp.float32)
+    correct = jnp.zeros((pooled.shape[0], 1), jnp.float32)
+    rival = jnp.full((pooled.shape[0], 1), -1e30, jnp.float32)
     for k in range(CLASSES):
         total = pooled[:, :128] * head[k, :, pl.ds(0, 128)]
         for j in range(1, 4):
             total = total + pooled[:, j * 128 : j * 128 + 128] * head[k, :, pl.ds(j * 128, 128)]
-        logits = jnp.where(lane == k, jnp.sum(total, axis=1, keepdims=True), logits)
-    chosen = lane == label
-    correct = jnp.sum(jnp.where(chosen, logits, 0.0), axis=1, keepdims=True)
-    rival = jnp.max(jnp.where(chosen, -1e30, logits), axis=1, keepdims=True)
+        logit = jnp.sum(total, axis=1, keepdims=True)
+        correct = jnp.where(label == k, logit, correct)
+        rival = jnp.where(label == k, rival, jnp.maximum(rival, logit))
     return correct - rival
 
 
@@ -93,7 +85,7 @@
         labels, head, ident, out = refs[:4]
     else:
         store = refs[0]
-    moved, hidden = refs[-2:]
+    moved, hidden, wide = refs[-3:]
     targets = moved.shape[1]
     deep = grids[0].shape[0]
     groups = targets // GROUP
@@ -101,9 +93,9 @@
 
     if last:
         core, y = lax.axis_index("core"), lax.axis_index("y")
-        wide = (targets, 128)
-        lane = lax.broadcasted_iota(jnp.int32, wide, 1)
-        line = lax.broadcasted_iota(jnp.int32, wide, 0)
+        lanes = (targets, 128)
+        lane = lax.broadcasted_iota(jnp.int32, lanes, 1)
+        line = lax.broadcasted_iota(jnp.int32, lanes, 0)
         few = labels.shape[1]
         spread_labels = jnp.broadcast_to(labels[...].astype(jnp.float32), (targets, few))
 
@@ -122,13 +114,7 @@
             for i in range(targets):
                 out[pl.ds(firsts[i // deep] + 2 * (i % deep), 1), 0, :] = packed[i : i + 1, :]
 
-    def shuffle(*flat):
-        by_position(sources, moved, (flat[:groups], flat[groups:]))
-
-    pl.run_scoped(
-        shuffle,
-        *[pltpu.ACC(n)((HALF, HALF), jnp.float32) for n in range(2) for _ in range(groups)],
-    )
+    by_position(sources, moved, wide)
     if last:
         for part in range(step):
             send(part, before[pl.ds(part * targets, targets), :])
@@ -188,6 +174,7 @@
         scratch_shapes=[
             pltpu.VMEM((SPOTS, targets, 512), jnp.bfloat16),
             pltpu.VMEM((SPOTS, targets, 512), jnp.bfloat16),
+            pltpu.VMEM((4, GROUP * SPOTS, 128), jnp.float32),
         ],
         input_output_aliases=aliases,
         cost_estimate=pl.CostEstimate(flops=work, bytes_accessed=1 << 20, transcendentals=0),
@@ -216,17 +203,21 @@
 def tail_kernel(columns, datamodel, mean_out, norm_out):
     models = columns.shape[0]
     rows = columns[:, 0, :]
+    turned = pltpu.roll(rows, 64, 1)
     lane = lax.broadcasted_iota(jnp.int32, rows.shape, 1)
-    margin = jnp.max(jnp.where(lane < 64, rows, -3e38), axis=1, keepdims=True)
-    ident = jnp.max(jnp.where(lane < 64, -1.0, rows), axis=1, keepdims=True)
+    margin = jnp.where(lane < 64, rows, turned)
+    ident = jnp.where(lane < 64, turned, rows)
     mean = jnp.sum(margin, axis=0, keepdims=True) / models
     centred = margin - mean
     norm = jnp.sqrt(1.0 + jnp.sum(centred * centred, axis=0, keepdims=True) / models)
     scaled = centred / norm
-    subset = lax.broadcasted_iota(jnp.int32, (models, SUBSETS), 1).astype(jnp.float32)
-    datamodel[...] = jnp.sum(jnp.where(subset == ident, scaled, 0.0), axis=0, keepdims=True)
-    mean_out[...] = jnp.broadcast_to(mean, mean_out.shape)
-    norm_out[...] = jnp.broadcast_to(norm, norm_out.shape)
+    for h in range(SUBSETS // 128):
+        subset = (lane + 128 * h).astype(jnp.float32)
+        datamodel[:, pl.ds(128 * h, 128)] = jnp.sum(
+            jnp.where(subset == ident, scaled, 0.0), axis=0, keepdims=True
+        )
+    mean_out[...] = mean
+    norm_out[...] = norm
 
 
 def tail_call(columns):

time: 53.9 us -> 53.7 us (level)
  no operation moved by 1% of the time
where the time goes in v2:
time: 53.7 us; the launch traced here: 53.5 us
  blocking collectives  31.6 us (59%)
  Pallas kernels  9.18 us (17%)
  starting transfers between devices  8.17 us (15%)
  waiting for transfers between devices  2.42 us (5%)
  between operations  1.39 us (3%)
  local copies, waits for them, and re-layouts  0.73 us (1%)
    all_to_all x2, blocking collectives, exchanged(): return lax.all_to_all(x, axis, 0, 0, tiled=True)  31.6 us
    pallas_call x4, Pallas kernels, conv_call(): pl.pallas_call(functools.partial(conv_kernel, columns, step, tail is not...  8.46 us
    ppermute x7, starting transfers between devices, swapped(): lax.ppermute(x, axis, [(i, i ^ mask) for i in range(lax.axis_size(axis))])  8.17 us
    ppermute x7, waiting for transfers between devices, swapped(): lax.ppermute(x, axis, [(i, i ^ mask) for i in range(lax.axis_size(axis))])  2.42 us
  transfers between devices with their start and end apart: 7, of which 1 were waited for; matrix products, arithmetic and copies ran while one was open for 0% of the time, Pallas kernels for 12%

profile of v2, /device:TPU:1, one launch (start us, length us, event | category | flops | bytes accessed | tf_op | source)
XLA Modules:
  0.0 53.5 jit_solution(8390843806622307818)
XLA Ops:
  0.6 0.0 copy-start.4
  0.6 0.7 %copy-done.4 = bf16[1,4,4,512]{3,2,1,0:T(4,128)(2,1)S(1)} copy-done((bf16[1,4,4,512]{3,2,1,0:T(4,128)(2,1)S(1)}, bf16[1,4,4,512]{3,2,1,0:T(4,128)(2,1)}, u32[]{:S(2)}) %copy-start.4) | copy-done | bytes 16408
  1.3 0.0 copy-start
  1.4 0.0 copy-start.1
  1.4 16.8 %all_to_all.10.refs_2_ = bf16[8,16,512]{2,1,0:T(8,128)(2,1)S(1)} all-to-all(bf16[8,16,512]{2,1,0:T(8,128)(2,1)S(1)} %spread.1), channel_id=1, replica_groups=mesh['y'=4,'z'=8,'core'=2,'dp'=4] {'z'}, dimensions={0} | all-to-all | bytes 262144 | tf_op jit(solution)/shard_map/all_to_all | solution.py:240
  18.2 2.3 %collective-permute-start.3 = (bf16[8,16,512]{2,1,0:T(8,128)(2,1)S(1)}, bf16[8,16,512]{2,1,0:T(8,128)(2,1)S(1)}, u32[]{:S(2)}, u32[]{:S(2)}) collective-permute-start(bf16[8,16,512]{2,1,0:T(8,128)(2,1)S(1)} %all_to_all.10.refs_2_), channel_id=1, source_target_pairs={{0,4},{4,0},{1,5},{5,1},{2,6},{6,2},{3,7},{7,3},{8,12},{12,8},{9,1... | collective-permute-start | bytes 393224 | tf_op jit(solution)/shard_map/ppermute | solution.py:244
  21.1 1.4 %collective-permute-start.1 = (bf16[8,16,512]{2,1,0:T(8,128)(2,1)S(1)}, bf16[8,16,512]{2,1,0:T(8,128)(2,1)S(1)}, u32[]{:S(2)}, u32[]{:S(2)}) collective-permute-start(bf16[8,16,512]{2,1,0:T(8,128)(2,1)S(1)} %all_to_all.10.refs_2_), channel_id=1, source_target_pairs={{0,64},{64,0},{128,192},{192,128},{1,65},{65,1},{129,193},{193,129... | collective-permute-start | bytes 393224 | tf_op jit(solution)/shard_map/ppermute | solution.py:244
  22.5 1.9 %collective-permute-start.2 = (bf16[8,16,512]{2,1,0:T(8,128)(2,1)S(1)}, bf16[8,16,512]{2,1,0:T(8,128)(2,1)S(1)}, u32[]{:S(2)}, u32[]{:S(2)}) collective-permute-start(bf16[8,16,512]{2,1,0:T(8,128)(2,1)S(1)} %all_to_all.10.refs_2_), channel_id=1, source_target_pairs={{0,192},{64,128},{128,64},{192,0},{1,193},{65,129},{129,65},{193,1... | collective-permute-start | bytes 393224 | tf_op jit(solution)/shard_map/ppermute | solution.py:244
  24.4 0.7 %collective-permute-start = (bf16[8,16,512]{2,1,0:T(8,128)(2,1)S(1)}, bf16[8,16,512]{2,1,0:T(8,128)(2,1)S(1)}, u32[]{:S(2)}, u32[]{:S(2)}) collective-permute-start(bf16[8,16,512]{2,1,0:T(8,128)(2,1)S(1)} %all_to_all.10.refs_2_), channel_id=1, source_target_pairs={{0,128},{64,192},{128,0},{192,64},{1,129},{65,193},{129,1},{193,65... | collective-permute-start | bytes 393224 | tf_op jit(solution)/shard_map/ppermute | solution.py:244
  25.1 0.0 collective-permute-done.3.refs_3_
  25.1 0.0 copy-done
  25.1 0.0 copy-done.1
  25.2 2.1 %shard_map.85.refs_4_ = f32[64,512]{1,0:T(8,128)S(1)} custom-call(bf16[9,512,512]{2,1,0:T(8,128)(2,1)S(1)} %bitcast.9, bf16[9,512,512]{2,1,0:T(8,128)(2,1)S(1)} %bitcast.13, bf16[8,16,512]{2,1,0:T(8,128)(2,1)S(1)} %all_to_all.10.refs_2_, bf16[8,16,512]{2,1,0:T(8,128)(2,1)S(1)} %collective-permute-done.3.refs_3_), custom_call_target="tpu_custom_call" | custom-call | flops 1677721600 | bytes 1048576 | tf_op jit(solution)/shard_map/pallas_call | solution.py:169
  27.2 0.0 collective-permute-done.1.refs_2_
  27.3 2.4 %collective-permute-done.2.refs_3_ = bf16[8,16,512]{2,1,0:T(8,128)(2,1)S(1)} collective-permute-done((bf16[8,16,512]{2,1,0:T(8,128)(2,1)S(1)}, bf16[8,16,512]{2,1,0:T(8,128)(2,1)S(1)}, u32[]{:S(2)}, u32[]{:S(2)}) %collective-permute-start.2) | collective-permute-done | bytes 131104 | tf_op jit(solution)/shard_map/ppermute | solution.py:244
  29.7 1.3 %collective-permute-start.5 = (bf16[8,16,512]{2,1,0:T(8,128)(2,1)S(1)}, bf16[8,16,512]{2,1,0:T(8,128)(2,1)S(1)}, u32[]{:S(2)}, u32[]{:S(2)}) collective-permute-start(bf16[8,16,512]{2,1,0:T(8,128)(2,1)S(1)} %collective-permute-done.1.refs_2_), channel_id=1, source_target_pairs={{0,4},{4,0},{1,5},{5,1},{2,6},{6,2},{3,7},{7,3},{8,12},{12,8},{9,1... | collective-permute-start | bytes 393224 | tf_op jit(solution)/shard_map/ppermute | solution.py:244
  30.9 0.0 collective-permute-start.6
  30.9 2.1 %shard_map.86.refs_4_ = f32[64,512]{1,0:T(8,128)S(1)} custom-call(bf16[9,512,512]{2,1,0:T(8,128)(2,1)S(1)} %bitcast.10, bf16[9,512,512]{2,1,0:T(8,128)(2,1)S(1)} %bitcast.14, bf16[8,16,512]{2,1,0:T(8,128)(2,1)S(1)} %collective-permute-done.1.refs_2_, bf16[8,16,512]{2,1,0:T(8,128)(2,1)S(1)} %collective-permute-done.2.refs_3_, ...), custom_call_target="tpu_custom_call", output_to_operand_aliasing={{}: (4, {})} | custom-call | flops 1677721600 | bytes 1048576 | tf_op jit(solution)/shard_map/pallas_call | solution.py:169
  33.0 0.0 copy-start.2
  33.1 0.0 copy-start.3
  33.1 0.0 collective-permute-done.refs_2_
  33.1 0.6 %collective-permute-start.4 = (bf16[8,16,512]{2,1,0:T(8,128)(2,1)S(1)}, bf16[8,16,512]{2,1,0:T(8,128)(2,1)S(1)}, u32[]{:S(2)}, u32[]{:S(2)}) collective-permute-start(bf16[8,16,512]{2,1,0:T(8,128)(2,1)S(1)} %collective-permute-done.refs_2_), channel_id=1, source_target_pairs={{0,4},{4,0},{1,5},{5,1},{2,6},{6,2},{3,7},{7,3},{8,12},{12,8},{9,1... | collective-permute-start | bytes 393224 | tf_op jit(solution)/shard_map/ppermute | solution.py:244
  33.7 0.0 collective-permute-done.5.refs_2_
  33.7 0.0 collective-permute-done.6.refs_3_
  33.7 2.1 %shard_map.87.refs_4_ = f32[64,512]{1,0:T(8,128)S(1)} custom-call(bf16[9,512,512]{2,1,0:T(8,128)(2,1)S(1)} %bitcast.11, bf16[9,512,512]{2,1,0:T(8,128)(2,1)S(1)} %bitcast.15, bf16[8,16,512]{2,1,0:T(8,128)(2,1)S(1)} %collective-permute-done.5.refs_2_, bf16[8,16,512]{2,1,0:T(8,128)(2,1)S(1)} %collective-permute-done.6.refs_3_, ...), custom_call_target="tpu_custom_call", output_to_operand_aliasing={{}: (4, {})} | custom-call | flops 1677721600 | bytes 1048576 | tf_op jit(solution)/shard_map/pallas_call | solution.py:169
  35.8 0.0 collective-permute-done.4.refs_3_
  35.8 0.0 copy-done.2
  35.8 0.0 copy-done.3
  35.8 2.2 %shard_map.88 = f32[64,1,128]{2,1,0:T(1,128)S(1)} custom-call(bf16[9,512,512]{2,1,0:T(8,128)(2,1)S(1)} %bitcast.12, bf16[9,512,512]{2,1,0:T(8,128)(2,1)S(1)} %bitcast.16, bf16[8,16,512]{2,1,0:T(8,128)(2,1)S(1)} %collective-permute-done.refs_2_, bf16[8,16,512]{2,1,0:T(8,128)(2,1)S(1)} %collective-permute-done.4.refs_3_, f32[64,512]{1,0:T(8,128)S(1)} %shard_map.87.refs_4_, ...), custom_call_target="tpu_custom_call" | custom-call | flops 1677721600 | bytes 1048576 | tf_op jit(solution)/shard_map/pallas_call | solution.py:169
  38.0 14.8 %all_to_all.11.columns = f32[64,1,128]{2,1,0:T(1,128)S(1)} all-to-all(f32[64,1,128]{2,1,0:T(1,128)S(1)} %shard_map.88), channel_id=1, replica_groups=mesh['y'=4,'z'=8,'core'=2,'dp'=4] {'y','z','core'}, dimensions={0} | all-to-all | bytes 65536 | tf_op jit(solution)/shard_map/all_to_all | solution.py:240
  52.8 0.7 %statistics.1 = (f32[1,256]{1,0:T(1,128)}, f32[1,128]{1,0:T(1,128)}, f32[1,128]{1,0:T(1,128)}) custom-call(f32[64,1,128]{2,1,0:T(1,128)S(1)} %all_to_all.11.columns), custom_call_target="tpu_custom_call" | custom-call | tf_op jit(solution)/shard_map/statistics/pallas_call | solution.py:225
  (1 shorter events, 0.0 us)
Async XLA Ops:
  0.6 0.7 %copy-start.4 = (bf16[1,4,4,512]{3,2,1,0:T(4,128)(2,1)S(1)}, bf16[1,4,4,512]{3,2,1,0:T(4,128)(2,1)}, u32[]{:S(2)}) copy-start(bf16[1,4,4,512]{3,2,1,0:T(4,128)(2,1)} %param.6) | copy-start | bytes 49156
  1.3 23.8 %copy-start = (bf16[1,9,512,512]{3,2,1,0:T(8,128)(2,1)S(1)}, bf16[1,9,512,512]{3,2,1,0:T(8,128)(2,1)}, u32[]{:S(2)}) copy-start(bf16[1,9,512,512]{3,2,1,0:T(8,128)(2,1)} %param.9) | copy-start | bytes 14155780
  1.4 23.8 %copy-start.1 = (bf16[1,9,512,512]{3,2,1,0:T(8,128)(2,1)S(1)}, bf16[1,9,512,512]{3,2,1,0:T(8,128)(2,1)}, u32[]{:S(2)}) copy-start(bf16[1,9,512,512]{3,2,1,0:T(8,128)(2,1)} %param.10) | copy-start | bytes 14155780
  18.2 7.0 %collective-permute-start.3 = (bf16[8,16,512]{2,1,0:T(8,128)(2,1)S(1)}, bf16[8,16,512]{2,1,0:T(8,128)(2,1)S(1)}, u32[]{:S(2)}, u32[]{:S(2)}) collective-permute-start(bf16[8,16,512]{2,1,0:T(8,128)(2,1)S(1)} %all_to_all.10.refs_2_), channel_id=1, source_target_pairs={{0,4},{4,0},{1,5},{5,1},{2,6},{6,2},{3,7},{7,3},{8,12},{12,8},{9,1... | collective-permute-start | bytes 393224 | tf_op jit(solution)/shard_map/ppermute | solution.py:244
  21.1 6.1 %collective-permute-start.1 = (bf16[8,16,512]{2,1,0:T(8,128)(2,1)S(1)}, bf16[8,16,512]{2,1,0:T(8,128)(2,1)S(1)}, u32[]{:S(2)}, u32[]{:S(2)}) collective-permute-start(bf16[8,16,512]{2,1,0:T(8,128)(2,1)S(1)} %all_to_all.10.refs_2_), channel_id=1, source_target_pairs={{0,64},{64,0},{128,192},{192,128},{1,65},{65,1},{129,193},{193,129... | collective-permute-start | bytes 393224 | tf_op jit(solution)/shard_map/ppermute | solution.py:244
  22.5 7.1 %collective-permute-start.2 = (bf16[8,16,512]{2,1,0:T(8,128)(2,1)S(1)}, bf16[8,16,512]{2,1,0:T(8,128)(2,1)S(1)}, u32[]{:S(2)}, u32[]{:S(2)}) collective-permute-start(bf16[8,16,512]{2,1,0:T(8,128)(2,1)S(1)} %all_to_all.10.refs_2_), channel_id=1, source_target_pairs={{0,192},{64,128},{128,64},{192,0},{1,193},{65,129},{129,65},{193,1... | collective-permute-start | bytes 393224 | tf_op jit(solution)/shard_map/ppermute | solution.py:244
  24.4 8.6 %collective-permute-start = (bf16[8,16,512]{2,1,0:T(8,128)(2,1)S(1)}, bf16[8,16,512]{2,1,0:T(8,128)(2,1)S(1)}, u32[]{:S(2)}, u32[]{:S(2)}) collective-permute-start(bf16[8,16,512]{2,1,0:T(8,128)(2,1)S(1)} %all_to_all.10.refs_2_), channel_id=1, source_target_pairs={{0,128},{64,192},{128,0},{192,64},{1,129},{65,193},{129,1},{193,65... | collective-permute-start | bytes 393224 | tf_op jit(solution)/shard_map/ppermute | solution.py:244
  29.7 4.0 %collective-permute-start.5 = (bf16[8,16,512]{2,1,0:T(8,128)(2,1)S(1)}, bf16[8,16,512]{2,1,0:T(8,128)(2,1)S(1)}, u32[]{:S(2)}, u32[]{:S(2)}) collective-permute-start(bf16[8,16,512]{2,1,0:T(8,128)(2,1)S(1)} %collective-permute-done.1.refs_2_), channel_id=1, source_target_pairs={{0,4},{4,0},{1,5},{5,1},{2,6},{6,2},{3,7},{7,3},{8,12},{12,8},{9,1... | collective-permute-start | bytes 393224 | tf_op jit(solution)/shard_map/ppermute | solution.py:244
  30.9 2.7 %collective-permute-start.6 = (bf16[8,16,512]{2,1,0:T(8,128)(2,1)S(1)}, bf16[8,16,512]{2,1,0:T(8,128)(2,1)S(1)}, u32[]{:S(2)}, u32[]{:S(2)}) collective-permute-start(bf16[8,16,512]{2,1,0:T(8,128)(2,1)S(1)} %collective-permute-done.2.refs_3_), channel_id=1, source_target_pairs={{0,4},{4,0},{1,5},{5,1},{2,6},{6,2},{3,7},{7,3},{8,12},{12,8},{9,1... | collective-permute-start | bytes 393224 | tf_op jit(solution)/shard_map/ppermute | solution.py:244
  33.0 2.7 %copy-start.2 = (f32[1,512,10]{1,0,2:T(1,128)S(1)}, f32[1,512,10]{1,0,2:T(1,128)}, u32[]{:S(2)}) copy-start(f32[1,512,10]{1,0,2:T(1,128)} %param.11) | copy-start | bytes 61444
  33.1 2.7 %copy-start.3 = (s32[64]{0:T(128)S(1)}, s32[64]{0:T(128)}, u32[]{:S(2)}) copy-start(s32[64]{0:T(128)} %param.7) | copy-start | bytes 772
  33.1 2.7 %collective-permute-start.4 = (bf16[8,16,512]{2,1,0:T(8,128)(2,1)S(1)}, bf16[8,16,512]{2,1,0:T(8,128)(2,1)S(1)}, u32[]{:S(2)}, u32[]{:S(2)}) collective-permute-start(bf16[8,16,512]{2,1,0:T(8,128)(2,1)S(1)} %collective-permute-done.refs_2_), channel_id=1, source_target_pairs={{0,4},{4,0},{1,5},{5,1},{2,6},{6,2},{3,7},{7,3},{8,12},{12,8},{9,1... | collective-permute-start | bytes 393224 | tf_op jit(solution)/shard_map/ppermute | solution.py:244

commit v3 on v2

--- a/solution.py
+++ b/solution.py
@@ -249,13 +249,13 @@
     head = jnp.transpose(head_weight, (2, 0, 1))
     fixed = (conv1_weight[0], conv2_weight[0])
     column_o = swapped(column, "core", 1)
-    near = swapped(column, "y", 1)
-    next_ = swapped(column, "y", 3)
+    near = swapped(column, "y", 3)
+    next_ = swapped(column, "y", 1)
     far = swapped(column, "y", 2)
     plan = (
         ((0, False), (0, True)),
-        ((1, False), (3, False)),
-        ((1, True), (3, True)),
+        ((3, False), (1, False)),
+        ((3, True), (1, True)),
         ((2, False), (2, True)),
     )
     pooled = conv_call(plan, 0, (column, column_o), *fixed)

time: 53.7 us -> 51.7 us (0.963)
  blocking collectives: 31.6 us -> 29.9 us
  waiting for transfers between devices: 2.42 us -> 1.4 us
  starting transfers between devices: 8.17 us -> 8.88 us
    all_to_all x2, blocking collectives: 31.6 us -> 29.9 us  [exchanged(): return lax.all_to_all(x, axis, 0, 0, tiled=True)]
    ppermute x7, waiting for transfers between devices: 2.42 us -> 1.4 us  [swapped(): lax.ppermute(x, axis, [(i, i ^ mask) for i in range(lax.axis_size(axis))])]
    ppermute x7, starting transfers between devices: 8.17 us -> 8.88 us  [swapped(): lax.ppermute(x, axis, [(i, i ^ mask) for i in range(lax.axis_size(axis))])]
  transfers between devices with their start and end apart: 7 -> 7, of which waited for: 1 -> 2; matrix products, arithmetic and copies ran while one was open for 0% -> 0% of each run, Pallas kernels for 12% -> 12%
where the time goes in v3:
time: 51.7 us; the launch traced here: 51.5 us
  blocking collectives  29.9 us (58%)
  Pallas kernels  9.16 us (18%)
  starting transfers between devices  8.88 us (17%)
  waiting for transfers between devices  1.4 us (3%)
  between operations  1.38 us (3%)
  local copies, waits for them, and re-layouts  0.73 us (1%)
    all_to_all x2, blocking collectives, exchanged(): return lax.all_to_all(x, axis, 0, 0, tiled=True)  29.9 us
    ppermute x7, starting transfers between devices, swapped(): lax.ppermute(x, axis, [(i, i ^ mask) for i in range(lax.axis_size(axis))])  8.88 us
    pallas_call x4, Pallas kernels, conv_call(): pl.pallas_call(functools.partial(conv_kernel, columns, step, tail is not...  8.45 us
    ppermute x7, waiting for transfers between devices, swapped(): lax.ppermute(x, axis, [(i, i ^ mask) for i in range(lax.axis_size(axis))])  1.4 us
  transfers between devices with their start and end apart: 7, of which 2 were waited for; matrix products, arithmetic and copies ran while one was open for 0% of the time, Pallas kernels for 12%

profile of v3, /device:TPU:1, one launch (start us, length us, event | category | flops | bytes accessed | tf_op | source)
XLA Modules:
  0.0 51.5 jit_solution(14962348519854453103)
XLA Ops:
  0.6 0.0 copy-start.4
  0.6 0.7 %copy-done.4 = bf16[1,4,4,512]{3,2,1,0:T(4,128)(2,1)S(1)} copy-done((bf16[1,4,4,512]{3,2,1,0:T(4,128)(2,1)S(1)}, bf16[1,4,4,512]{3,2,1,0:T(4,128)(2,1)}, u32[]{:S(2)}) %copy-start.4) | copy-done | bytes 16408
  1.3 0.0 copy-start
  1.4 0.0 copy-start.1
  1.4 16.8 %all_to_all.10.refs_2_ = bf16[8,16,512]{2,1,0:T(8,128)(2,1)S(1)} all-to-all(bf16[8,16,512]{2,1,0:T(8,128)(2,1)S(1)} %spread.1), channel_id=1, replica_groups=mesh['y'=4,'z'=8,'core'=2,'dp'=4] {'z'}, dimensions={0} | all-to-all | bytes 262144 | tf_op jit(solution)/shard_map/all_to_all | solution.py:240
  18.2 2.3 %collective-permute-start.3 = (bf16[8,16,512]{2,1,0:T(8,128)(2,1)S(1)}, bf16[8,16,512]{2,1,0:T(8,128)(2,1)S(1)}, u32[]{:S(2)}, u32[]{:S(2)}) collective-permute-start(bf16[8,16,512]{2,1,0:T(8,128)(2,1)S(1)} %all_to_all.10.refs_2_), channel_id=1, source_target_pairs={{0,4},{4,0},{1,5},{5,1},{2,6},{6,2},{3,7},{7,3},{8,12},{12,8},{9,1... | collective-permute-start | bytes 393224 | tf_op jit(solution)/shard_map/ppermute | solution.py:244
  21.1 2.8 %collective-permute-start.1 = (bf16[8,16,512]{2,1,0:T(8,128)(2,1)S(1)}, bf16[8,16,512]{2,1,0:T(8,128)(2,1)S(1)}, u32[]{:S(2)}, u32[]{:S(2)}) collective-permute-start(bf16[8,16,512]{2,1,0:T(8,128)(2,1)S(1)} %all_to_all.10.refs_2_), channel_id=1, source_target_pairs={{0,192},{64,128},{128,64},{192,0},{1,193},{65,129},{129,65},{193,1... | collective-permute-start | bytes 393224 | tf_op jit(solution)/shard_map/ppermute | solution.py:244
  24.0 0.0 collective-permute-start.2
  24.0 1.3 %collective-permute-start = (bf16[8,16,512]{2,1,0:T(8,128)(2,1)S(1)}, bf16[8,16,512]{2,1,0:T(8,128)(2,1)S(1)}, u32[]{:S(2)}, u32[]{:S(2)}) collective-permute-start(bf16[8,16,512]{2,1,0:T(8,128)(2,1)S(1)} %all_to_all.10.refs_2_), channel_id=1, source_target_pairs={{0,128},{64,192},{128,0},{192,64},{1,129},{65,193},{129,1},{193,65... | collective-permute-start | bytes 393224 | tf_op jit(solution)/shard_map/ppermute | solution.py:244
  25.2 0.0 collective-permute-done.3.refs_3_
  25.2 0.0 copy-done
  25.2 0.0 copy-done.1
  25.3 2.1 %shard_map.85.refs_4_ = f32[64,512]{1,0:T(8,128)S(1)} custom-call(bf16[9,512,512]{2,1,0:T(8,128)(2,1)S(1)} %bitcast.9, bf16[9,512,512]{2,1,0:T(8,128)(2,1)S(1)} %bitcast.13, bf16[8,16,512]{2,1,0:T(8,128)(2,1)S(1)} %all_to_all.10.refs_2_, bf16[8,16,512]{2,1,0:T(8,128)(2,1)S(1)} %collective-permute-done.3.refs_3_), custom_call_target="tpu_custom_call" | custom-call | flops 1677721600 | bytes 1048576 | tf_op jit(solution)/shard_map/pallas_call | solution.py:169
  27.3 0.3 collective-permute-done.1.refs_2_
  27.6 1.1 %collective-permute-done.2.refs_3_ = bf16[8,16,512]{2,1,0:T(8,128)(2,1)S(1)} collective-permute-done((bf16[8,16,512]{2,1,0:T(8,128)(2,1)S(1)}, bf16[8,16,512]{2,1,0:T(8,128)(2,1)S(1)}, u32[]{:S(2)}, u32[]{:S(2)}) %collective-permute-start.2) | collective-permute-done | bytes 131104 | tf_op jit(solution)/shard_map/ppermute | solution.py:244
  28.7 1.9 %collective-permute-start.5 = (bf16[8,16,512]{2,1,0:T(8,128)(2,1)S(1)}, bf16[8,16,512]{2,1,0:T(8,128)(2,1)S(1)}, u32[]{:S(2)}, u32[]{:S(2)}) collective-permute-start(bf16[8,16,512]{2,1,0:T(8,128)(2,1)S(1)} %collective-permute-done.1.refs_2_), channel_id=1, source_target_pairs={{0,4},{4,0},{1,5},{5,1},{2,6},{6,2},{3,7},{7,3},{8,12},{12,8},{9,1... | collective-permute-start | bytes 393224 | tf_op jit(solution)/shard_map/ppermute | solution.py:244
  30.6 0.0 collective-permute-start.6
  30.6 2.1 %shard_map.86.refs_4_ = f32[64,512]{1,0:T(8,128)S(1)} custom-call(bf16[9,512,512]{2,1,0:T(8,128)(2,1)S(1)} %bitcast.10, bf16[9,512,512]{2,1,0:T(8,128)(2,1)S(1)} %bitcast.14, bf16[8,16,512]{2,1,0:T(8,128)(2,1)S(1)} %collective-permute-done.1.refs_2_, bf16[8,16,512]{2,1,0:T(8,128)(2,1)S(1)} %collective-permute-done.2.refs_3_, ...), custom_call_target="tpu_custom_call", output_to_operand_aliasing={{}: (4, {})} | custom-call | flops 1677721600 | bytes 1048576 | tf_op jit(solution)/shard_map/pallas_call | solution.py:169
  32.7 0.0 copy-start.2
  32.7 0.0 copy-start.3
  32.7 0.0 collective-permute-done.refs_2_
  32.7 0.6 %collective-permute-start.4 = (bf16[8,16,512]{2,1,0:T(8,128)(2,1)S(1)}, bf16[8,16,512]{2,1,0:T(8,128)(2,1)S(1)}, u32[]{:S(2)}, u32[]{:S(2)}) collective-permute-start(bf16[8,16,512]{2,1,0:T(8,128)(2,1)S(1)} %collective-permute-done.refs_2_), channel_id=1, source_target_pairs={{0,4},{4,0},{1,5},{5,1},{2,6},{6,2},{3,7},{7,3},{8,12},{12,8},{9,1... | collective-permute-start | bytes 393224 | tf_op jit(solution)/shard_map/ppermute | solution.py:244
  33.3 0.0 collective-permute-done.5.refs_2_
  33.3 0.0 collective-permute-done.6.refs_3_
  33.3 2.1 %shard_map.87.refs_4_ = f32[64,512]{1,0:T(8,128)S(1)} custom-call(bf16[9,512,512]{2,1,0:T(8,128)(2,1)S(1)} %bitcast.11, bf16[9,512,512]{2,1,0:T(8,128)(2,1)S(1)} %bitcast.15, bf16[8,16,512]{2,1,0:T(8,128)(2,1)S(1)} %collective-permute-done.5.refs_2_, bf16[8,16,512]{2,1,0:T(8,128)(2,1)S(1)} %collective-permute-done.6.refs_3_, ...), custom_call_target="tpu_custom_call", output_to_operand_aliasing={{}: (4, {})} | custom-call | flops 1677721600 | bytes 1048576 | tf_op jit(solution)/shard_map/pallas_call | solution.py:169
  35.4 0.0 collective-permute-done.4.refs_3_
  35.4 0.0 copy-done.2
  35.5 0.0 copy-done.3
  35.5 2.2 %shard_map.88 = f32[64,1,128]{2,1,0:T(1,128)S(1)} custom-call(bf16[9,512,512]{2,1,0:T(8,128)(2,1)S(1)} %bitcast.12, bf16[9,512,512]{2,1,0:T(8,128)(2,1)S(1)} %bitcast.16, bf16[8,16,512]{2,1,0:T(8,128)(2,1)S(1)} %collective-permute-done.refs_2_, bf16[8,16,512]{2,1,0:T(8,128)(2,1)S(1)} %collective-permute-done.4.refs_3_, f32[64,512]{1,0:T(8,128)S(1)} %shard_map.87.refs_4_, ...), custom_call_target="tpu_custom_call" | custom-call | flops 1677721600 | bytes 1048576 | tf_op jit(solution)/shard_map/pallas_call | solution.py:169
  37.7 13.1 %all_to_all.11.columns = f32[64,1,128]{2,1,0:T(1,128)S(1)} all-to-all(f32[64,1,128]{2,1,0:T(1,128)S(1)} %shard_map.88), channel_id=1, replica_groups=mesh['y'=4,'z'=8,'core'=2,'dp'=4] {'y','z','core'}, dimensions={0} | all-to-all | bytes 65536 | tf_op jit(solution)/shard_map/all_to_all | solution.py:240
  50.8 0.7 %statistics.1 = (f32[1,256]{1,0:T(1,128)}, f32[1,128]{1,0:T(1,128)}, f32[1,128]{1,0:T(1,128)}) custom-call(f32[64,1,128]{2,1,0:T(1,128)S(1)} %all_to_all.11.columns), custom_call_target="tpu_custom_call" | custom-call | tf_op jit(solution)/shard_map/statistics/pallas_call | solution.py:225
  (1 shorter events, 0.0 us)
Async XLA Ops:
  0.6 0.7 %copy-start.4 = (bf16[1,4,4,512]{3,2,1,0:T(4,128)(2,1)S(1)}, bf16[1,4,4,512]{3,2,1,0:T(4,128)(2,1)}, u32[]{:S(2)}) copy-start(bf16[1,4,4,512]{3,2,1,0:T(4,128)(2,1)} %param.6) | copy-start | bytes 49156
  1.3 23.9 %copy-start = (bf16[1,9,512,512]{3,2,1,0:T(8,128)(2,1)S(1)}, bf16[1,9,512,512]{3,2,1,0:T(8,128)(2,1)}, u32[]{:S(2)}) copy-start(bf16[1,9,512,512]{3,2,1,0:T(8,128)(2,1)} %param.9) | copy-start | bytes 14155780
  1.4 23.9 %copy-start.1 = (bf16[1,9,512,512]{3,2,1,0:T(8,128)(2,1)S(1)}, bf16[1,9,512,512]{3,2,1,0:T(8,128)(2,1)}, u32[]{:S(2)}) copy-start(bf16[1,9,512,512]{3,2,1,0:T(8,128)(2,1)} %param.10) | copy-start | bytes 14155780
  18.2 7.1 %collective-permute-start.3 = (bf16[8,16,512]{2,1,0:T(8,128)(2,1)S(1)}, bf16[8,16,512]{2,1,0:T(8,128)(2,1)S(1)}, u32[]{:S(2)}, u32[]{:S(2)}) collective-permute-start(bf16[8,16,512]{2,1,0:T(8,128)(2,1)S(1)} %all_to_all.10.refs_2_), channel_id=1, source_target_pairs={{0,4},{4,0},{1,5},{5,1},{2,6},{6,2},{3,7},{7,3},{8,12},{12,8},{9,1... | collective-permute-start | bytes 393224 | tf_op jit(solution)/shard_map/ppermute | solution.py:244
  21.1 6.5 %collective-permute-start.1 = (bf16[8,16,512]{2,1,0:T(8,128)(2,1)S(1)}, bf16[8,16,512]{2,1,0:T(8,128)(2,1)S(1)}, u32[]{:S(2)}, u32[]{:S(2)}) collective-permute-start(bf16[8,16,512]{2,1,0:T(8,128)(2,1)S(1)} %all_to_all.10.refs_2_), channel_id=1, source_target_pairs={{0,192},{64,128},{128,64},{192,0},{1,193},{65,129},{129,65},{193,1... | collective-permute-start | bytes 393224 | tf_op jit(solution)/shard_map/ppermute | solution.py:244
  24.0 4.8 %collective-permute-start.2 = (bf16[8,16,512]{2,1,0:T(8,128)(2,1)S(1)}, bf16[8,16,512]{2,1,0:T(8,128)(2,1)S(1)}, u32[]{:S(2)}, u32[]{:S(2)}) collective-permute-start(bf16[8,16,512]{2,1,0:T(8,128)(2,1)S(1)} %all_to_all.10.refs_2_), channel_id=1, source_target_pairs={{0,64},{64,0},{128,192},{192,128},{1,65},{65,1},{129,193},{193,129... | collective-permute-start | bytes 393224 | tf_op jit(solution)/shard_map/ppermute | solution.py:244
  24.0 8.8 %collective-permute-start = (bf16[8,16,512]{2,1,0:T(8,128)(2,1)S(1)}, bf16[8,16,512]{2,1,0:T(8,128)(2,1)S(1)}, u32[]{:S(2)}, u32[]{:S(2)}) collective-permute-start(bf16[8,16,512]{2,1,0:T(8,128)(2,1)S(1)} %all_to_all.10.refs_2_), channel_id=1, source_target_pairs={{0,128},{64,192},{128,0},{192,64},{1,129},{65,193},{129,1},{193,65... | collective-permute-start | bytes 393224 | tf_op jit(solution)/shard_map/ppermute | solution.py:244
  28.7 4.6 %collective-permute-start.5 = (bf16[8,16,512]{2,1,0:T(8,128)(2,1)S(1)}, bf16[8,16,512]{2,1,0:T(8,128)(2,1)S(1)}, u32[]{:S(2)}, u32[]{:S(2)}) collective-permute-start(bf16[8,16,512]{2,1,0:T(8,128)(2,1)S(1)} %collective-permute-done.1.refs_2_), channel_id=1, source_target_pairs={{0,4},{4,0},{1,5},{5,1},{2,6},{6,2},{3,7},{7,3},{8,12},{12,8},{9,1... | collective-permute-start | bytes 393224 | tf_op jit(solution)/shard_map/ppermute | solution.py:244
  30.6 2.7 %collective-permute-start.6 = (bf16[8,16,512]{2,1,0:T(8,128)(2,1)S(1)}, bf16[8,16,512]{2,1,0:T(8,128)(2,1)S(1)}, u32[]{:S(2)}, u32[]{:S(2)}) collective-permute-start(bf16[8,16,512]{2,1,0:T(8,128)(2,1)S(1)} %collective-permute-done.2.refs_3_), channel_id=1, source_target_pairs={{0,4},{4,0},{1,5},{5,1},{2,6},{6,2},{3,7},{7,3},{8,12},{12,8},{9,1... | collective-permute-start | bytes 393224 | tf_op jit(solution)/shard_map/ppermute | solution.py:244
  32.7 2.7 %copy-start.2 = (f32[1,512,10]{1,0,2:T(1,128)S(1)}, f32[1,512,10]{1,0,2:T(1,128)}, u32[]{:S(2)}) copy-start(f32[1,512,10]{1,0,2:T(1,128)} %param.11) | copy-start | bytes 61444
  32.7 2.7 %copy-start.3 = (s32[64]{0:T(128)S(1)}, s32[64]{0:T(128)}, u32[]{:S(2)}) copy-start(s32[64]{0:T(128)} %param.7) | copy-start | bytes 772
  32.7 2.7 %collective-permute-start.4 = (bf16[8,16,512]{2,1,0:T(8,128)(2,1)S(1)}, bf16[8,16,512]{2,1,0:T(8,128)(2,1)S(1)}, u32[]{:S(2)}, u32[]{:S(2)}) collective-permute-start(bf16[8,16,512]{2,1,0:T(8,128)(2,1)S(1)} %collective-permute-done.refs_2_), channel_id=1, source_target_pairs={{0,4},{4,0},{1,5},{5,1},{2,6},{6,2},{3,7},{7,3},{8,12},{12,8},{9,1... | collective-permute-start | bytes 393224 | tf_op jit(solution)/shard_map/ppermute | solution.py:244
